TPU v7x, 256 devices: a whole 4x4x8 slice. The times are simulated.
256 devices in a mesh: seq: 64 (over z, x, core), kvh: 4 (over y).
Axes of the slice: x: 4, y: 4, z: 8, core: 2. Of those that a mesh axis runs over, the one named last changes fastest.
Arguments:
- queries: bfloat16 [8192, 28, 128], P('seq', 'kvh'), may hold values from -80 to 80
- new_keys: bfloat16 [8192, 4, 128], P('seq', 'kvh'), may hold values from -8 to 8
- cache_keys: bfloat16 [4096, 4, 128], P('seq', 'kvh'), may hold values from -1.1953125 to 1.1953125
- window_start: int32 [64], replicated, may hold values from 0 to 7680, as said below
- owner_slot: int32 [64], replicated, may hold values from 0 to 4095, as said below
Outputs:
- relevance: bfloat16 [8192, 28, 4096], P('seq', 'kvh')
- rep_bank: bfloat16 [4096, 4, 128], P('seq', 'kvh')
Inputs may be any that keep to these rules, and one draw needn't show every extreme that they name: `window_start`: each window lies inside the new tokens; some window begins at the first new token and some ends at the last. `owner_slot`: the slots are distinct; the first and the last memory block are always among them.
All inputs are finite; a program needn't handle non-finite values.
Results may differ from a plain program's by a relative error of at most 0.0018.
Values may be sent and summed in bfloat16 or wider, within the bound.
A program may use at most 64 MiB of HBM per device.

v0:
```python
import math

import jax
import jax.numpy as jnp
from jax import lax
from jax.sharding import Mesh
from jax.sharding import PartitionSpec as P

BLK = 128
WIN = 512
SEQ = ("seq_0", "seq_1", "seq_2")


def copy_for_each(shard, axis):
    devices = lax.axis_size(axis)
    return lax.all_to_all(
        jnp.broadcast_to(shard[None], (devices, *shard.shape)), axis, 0, 0, tiled=True
    )


def in_order(tiles, dim):
    tiles = jnp.moveaxis(tiles, 0, dim)
    shape = tiles.shape
    return tiles.reshape(*shape[:dim], shape[dim] * shape[dim + 1], *shape[dim + 2 :])


def gather_axes(shard, axes, dim):
    far, near = axes
    tiles = copy_for_each(copy_for_each(shard, far), near)
    return in_order(tiles.swapaxes(0, 1).reshape(-1, *shard.shape), dim)


def split_up(shard, dim, devices):
    shape = shard.shape
    tiles = shard.reshape(*shape[:dim], devices, shape[dim] // devices, *shape[dim + 1 :])
    return jnp.moveaxis(tiles, dim, 0)


def sum_at_owner(shard, axis, dim):
    tiles = split_up(shard, dim, lax.axis_size(axis))
    arrived = lax.all_to_all(tiles, axis, split_axis=0, concat_axis=0, tiled=True)
    return arrived.sum(axis=0)


def padded_to(lines, devices):
    spare = -len(lines) % devices
    return jnp.pad(lines, [(0, spare)] + [(0, 0)] * (lines.ndim - 1))


def collect(shard, axis, dim):
    tiles = copy_for_each(shard, axis)
    return in_order(tiles, dim)


def sum_by_parts(shard, axes):
    lines = shard.reshape(-1, shard.shape[-1])
    own = sum_at_owner(padded_to(lines, lax.axis_size(axes)), axes, 0)
    whole = collect(own, axes, 0)
    return whole[: len(lines)].reshape(shard.shape)


def row_scores(query_rows, key_rows):
    return lax.dot_general(
        query_rows, key_rows, (((1,), (1,)), ((), ())), preferred_element_type=jnp.float32
    )


def per_device(queries, new_keys, cache_keys, window_start, owner_slot):
    tok_count, group_size, head_dim = queries.shape
    score_scale = 1.0 / math.sqrt(head_dim)
    query_rows = queries.reshape(tok_count * group_size, head_dim)
    device_index = lax.axis_index(SEQ)
    keys_all, bank_old = (
        gather_axes(new_keys, (("seq_0", "seq_1"), "seq_2"), 0),
        gather_axes(cache_keys, (("seq_0", "seq_1"), "seq_2"), 0),
    )
    key_flat = keys_all[:, 0, :]
    total_tokens = key_flat.shape[0]
    block_count = total_tokens // BLK
    group_blocks = math.gcd(block_count, 8)
    position = device_index * tok_count + jnp.arange(tok_count, dtype=jnp.int32)
    row_position = jnp.repeat(position, group_size)
    inside = (row_position[:, None] >= window_start[None, :]) & (
        row_position[:, None] < window_start[None, :] + WIN
    )
    inside = inside.astype(jnp.float32)
    key_groups = key_flat.reshape(block_count // group_blocks, group_blocks * BLK, head_dim)
    inside_groups = inside.reshape(
        query_rows.shape[0], block_count // group_blocks, group_blocks
    ).transpose(1, 0, 2)

    def group_sums(members):
        key_part, mask_part = members
        scores = row_scores(query_rows, key_part) * score_scale
        scores = scores.reshape(query_rows.shape[0], group_blocks, BLK)
        softmax_weights = jax.nn.softmax(scores, axis=-1)
        return jnp.einsum("rgk,rg->gk", softmax_weights, mask_part)

    colsum = lax.map(group_sums, (key_groups, inside_groups)).reshape(block_count, BLK)
    colsum = sum_by_parts(colsum, SEQ)
    weights = colsum / (group_size * WIN)
    representative = jnp.einsum(
        "nr,nrz->nz",
        weights,
        key_flat.reshape(block_count, BLK, head_dim).astype(jnp.float32),
        precision=lax.Precision.HIGHEST,
    ).astype(jnp.bfloat16)
    rep_float = representative.astype(jnp.float32)
    local_blocks = cache_keys.shape[0]
    slot_ids = device_index * local_blocks + jnp.arange(local_blocks, dtype=jnp.int32)
    matches = (owner_slot[:, None] == slot_ids[None, :]).astype(jnp.float32)
    placed = jnp.dot(matches.T, rep_float, precision=lax.Precision.HIGHEST)
    slot_taken = jnp.sum(matches, axis=0) > 0.5
    new_shard = jnp.where(slot_taken[:, None], placed.astype(jnp.bfloat16), cache_keys[:, 0, :])
    bank_rows = bank_old[:, 0, :]
    every_slot = jnp.arange(bank_rows.shape[0], dtype=jnp.int32)
    matches_all = (owner_slot[:, None] == every_slot[None, :]).astype(jnp.float32)
    placed_all = jnp.dot(matches_all.T, rep_float, precision=lax.Precision.HIGHEST)
    taken_all = jnp.sum(matches_all, axis=0) > 0.5
    key_bank = jnp.where(taken_all[:, None], placed_all.astype(jnp.bfloat16), bank_rows)
    totals = row_scores(query_rows, key_bank) * score_scale
    relevance = totals.astype(jnp.bfloat16).reshape(tok_count, group_size, totals.shape[1])
    return (relevance, new_shard[:, None, :])


def solution(mesh):
    finer = Mesh(
        mesh.devices.reshape(8, 4, 2, mesh.shape["kvh"]), ("seq_0", "seq_1", "seq_2", "kvh")
    )
    in_specs = (P(SEQ, "kvh", None), P(SEQ, "kvh", None), P(SEQ, "kvh", None), P(), P())
    out_specs = (P(SEQ, "kvh", None), P(SEQ, "kvh", None))
    return jax.shard_map(
        per_device, mesh=finer, in_specs=in_specs, out_specs=out_specs, check_vma=False
    )
```

profile of v0, /device:TPU:1, one launch (start us, length us, event | category | flops | bytes accessed | tf_op | source)
XLA Modules:
  0.0 153.2 jit_solution(7968012248715033259)
XLA Ops:
  0.6 2.0 %broadcast_in_dim.80 = bf16[32,128,1,128]{3,1,2,0:T(8,128)(2,1)} broadcast(bf16[128,128]{1,0:T(8,128)(2,1)} %bitcast.77), dimensions={1,3} | broadcast | bytes 1081344 | tf_op jit(solution)/shard_map/broadcast_in_dim | solution.py:17
  2.6 11.9 %all-to-all-start = ((bf16[32,128,1,128]{3,1,2,0:T(8,128)(2,1)}), bf16[32,128,1,128]{3,1,2,0:T(8,128)(2,1)S(1)}, u32[]{:S(2)}, u32[]{:S(2)}) async-start(bf16[32,128,1,128]{3,1,2,0:T(8,128)(2,1)} %broadcast_in_dim.80), calls=%async_computation | async-start | bytes 2097152 | tf_op jit(solution)/shard_map/all_to_all | solution.py:16
  16.3 1.1 copy.19
  17.8 22.9 %all-to-all-done = bf16[32,128,1,128]{3,1,2,0:T(8,128)(2,1)S(1)} async-done(((bf16[32,128,1,128]{3,1,2,0:T(8,128)(2,1)}), bf16[32,128,1,128]{3,1,2,0:T(8,128)(2,1)S(1)}, u32[]{:S(2)}, u32[]{:S(2)}) %all-to-all-start) | async-done | bytes 1048608 | tf_op jit(solution)/shard_map/all_to_all | solution.py:16
  41.2 8.7 %all_to_all.30 = bf16[2,32,128,1,128]{4,2,1,3,0:T(8,128)(2,1)} all-to-all(bf16[2,32,128,1,128]{4,2,1,3,0:T(8,128)(2,1)S(1)} %broadcast_in_dim.82), channel_id=1, replica_groups=mesh['seq_0'=8,'seq_1'=4,'seq_2'=2,'kvh'=4] {'seq_2'}, dimensions={0} | all-to-all | bytes 4194304 | tf_op jit(solution)/shard_map/all_to_all | solution.py:16
  49.9 0.9 broadcast_in_dim.86
  50.8 5.3 %all-to-all-start.4 = ((bf16[32,64,1,128]{3,1,2,0:T(8,128)(2,1)}), bf16[32,64,1,128]{3,1,2,0:T(8,128)(2,1)S(1)}, u32[]{:S(2)}, u32[]{:S(2)}) async-start(bf16[32,64,1,128]{3,1,2,0:T(8,128)(2,1)} %broadcast_in_dim.86), calls=%async_computation.4 | async-start | bytes 1048576 | tf_op jit(solution)/shard_map/all_to_all | solution.py:16
  56.1 1.7 %copy.18 = bf16[2,32,128,1,128]{4,2,0,1,3:T(8,128)(2,1)S(1)} copy(bf16[2,32,128,1,128]{4,2,1,3,0:T(8,128)(2,1)} %all_to_all.30) | data formatting | bytes 4194304 | tf_op jit(solution)/shard_map/all_to_all | solution.py:16
  57.9 23.9 %while.10 = (s32[]{:T(128)}, f32[8,8,128]{2,1,0:T(8,128)}, bf16[8,1024,128]{2,1,0:T(8,128)(2,1)S(1)}, bf16[896,128]{1,0:T(8,128)(2,1)S(1)}, bf16[8,896,8]{1,2,0:T(8,128)(2,1)S(1)}, /*index=5*/s32[]{:T(128)}, f32[]{:T(128)}) while((s32[]{:T(128)}, f32[8,8,128]{2,1,0:T(8,128)}, bf16[8,1024,128]{2,1,0:T(8,128)(2,1)S(1)}, ...), condition=%wide.region_4.5_spmd, body=%wide.region_1.4_spmd.sunk | while | flops 244041728 | bytes 19040356 | solution.py:99
  65.4 0.8 fusion.41
  81.7 10.6 %all-to-all-start.2 = ((f32[64,1,128]{2,1,0:T(1,128)}), f32[64,1,128]{2,1,0:T(1,128)S(1)}, u32[]{:S(2)}, u32[]{:S(2)}) async-start(f32[64,1,128]{2,1,0:T(1,128)} %bitcast.13), calls=%async_computation.2 | async-start | bytes 65536 | tf_op jit(solution)/shard_map/all_to_all | solution.py:41
  92.4 9.3 %all-to-all-done.2 = f32[64,1,128]{2,1,0:T(1,128)S(1)} async-done(((f32[64,1,128]{2,1,0:T(1,128)}), f32[64,1,128]{2,1,0:T(1,128)S(1)}, u32[]{:S(2)}, u32[]{:S(2)}) %all-to-all-start.2) | async-done | bytes 32800 | tf_op jit(solution)/shard_map/all_to_all | solution.py:41
  101.8 1.3 broadcast_in_dim.88
  103.1 4.2 %all-to-all-start.5 = ((bf16[2,32,64,1,128]{4,2,1,3,0:T(8,128)(2,1)}), bf16[2,32,64,1,128]{4,2,1,3,0:T(8,128)(2,1)S(1)}, u32[]{:S(2)}, u32[]{:S(2)}) async-start(bf16[2,32,64,1,128]{4,2,1,3,0:T(8,128)(2,1)} %broadcast_in_dim.88), calls=%async_computation.5 | async-start | bytes 2097152 | tf_op jit(solution)/shard_map/all_to_all | solution.py:16
  107.4 1.7 %all-to-all-done.5 = bf16[2,32,64,1,128]{4,2,1,3,0:T(8,128)(2,1)S(1)} async-done(((bf16[2,32,64,1,128]{4,2,1,3,0:T(8,128)(2,1)}), bf16[2,32,64,1,128]{4,2,1,3,0:T(8,128)(2,1)S(1)}, u32[]{:S(2)}, u32[]{:S(2)}) %all-to-all-start.5) | async-done | bytes 1048608 | tf_op jit(solution)/shard_map/all_to_all | solution.py:16
  109.7 4.4 %all-to-all-start.3 = ((f32[64,1,128]{2,1,0:T(1,128)}), f32[64,1,128]{2,1,0:T(1,128)S(1)}, u32[]{:S(2)}, u32[]{:S(2)}) async-start(f32[64,1,128]{2,1,0:T(1,128)} %broadcast_in_dim.84), calls=%async_computation.3 | async-start | bytes 65536 | tf_op jit(solution)/shard_map/all_to_all | solution.py:16
  114.1 1.3 copy.20
  115.4 8.2 %all-to-all-done.3 = f32[64,1,128]{2,1,0:T(1,128)S(1)} async-done(((f32[64,1,128]{2,1,0:T(1,128)}), f32[64,1,128]{2,1,0:T(1,128)S(1)}, u32[]{:S(2)}, u32[]{:S(2)}) %all-to-all-start.3) | async-done | bytes 32800 | tf_op jit(solution)/shard_map/all_to_all | solution.py:16
  123.6 1.7 %fusion.19 = f32[64,1,128]{2,1,0:T(1,128)S(1)} fusion(bf16[64,128,128]{2,1,0:T(8,128)(2,1)S(1)} %bitcast.69, f32[64,1,128]{2,1,0:T(1,128)S(1)} %all-to-all-done.3), kind=kOutput, calls=%fused_computation.29 | convolution fusion | flops 12591104 | bytes 2162688 | tf_op jit(solution)/shard_map/nr,nrz->nz/dot_general | solution.py:102
  125.3 0.9 fusion.15
  126.2 1.4 fusion.13
  127.6 5.1 %fusion.12 = bf16[896,4096]{1,0:T(8,128)(2,1)} fusion(bf16[4096,128]{1,0:T(8,128)(2,1)S(1)} %fusion.13, bf16[896,128]{1,0:T(8,128)(2,1)S(1)} %get-tuple-element.109), kind=kOutput, calls=%fused_computation.16 | convolution fusion | flops 946864128 | bytes 8617984 | tf_op jit(solution)/shard_map/dot_general | solution.py:63
  132.8 9.4 %reshape.78 = bf16[128,7,4096]{2,1,0:T(8,128)(2,1)} reshape(bf16[896,4096]{1,0:T(8,128)(2,1)} %fusion.12) | data formatting | bytes 14680064 | tf_op jit(solution)/shard_map/reshape | solution.py:122
  142.2 11.0 %copy.21 = bf16[128,7,4096]{2,0,1:T(8,128)(2,1)} copy(bf16[128,7,4096]{2,1,0:T(8,128)(2,1)} %reshape.78) | data formatting | bytes 14680064
  (71 shorter events, 26.4 us)
Async XLA Ops:
  0.6 16.8 %copy-start.2 = (s32[64]{0:T(128)S(1)}, s32[64]{0:T(128)}, u32[]{:S(2)}) copy-start(s32[64]{0:T(128)} %param.11) | copy-start | bytes 772
  2.6 38.1 %all-to-all-start = ((bf16[32,128,1,128]{3,1,2,0:T(8,128)(2,1)}), bf16[32,128,1,128]{3,1,2,0:T(8,128)(2,1)S(1)}, u32[]{:S(2)}, u32[]{:S(2)}) async-start(bf16[32,128,1,128]{3,1,2,0:T(8,128)(2,1)} %broadcast_in_dim.80), calls=%async_computation | async-start | bytes 2097152 | tf_op jit(solution)/shard_map/all_to_all | solution.py:16
  40.7 9.3 %copy-start.1 = (bf16[64,1,128]{2,0,1:T(8,128)(2,1)S(1)}, bf16[64,1,128]{2,0,1:T(8,128)(2,1)}, u32[]{:S(2)}) copy-start(bf16[64,1,128]{2,0,1:T(8,128)(2,1)} %param.9) | copy-start | bytes 49156
  50.8 30.9 %all-to-all-start.4 = ((bf16[32,64,1,128]{3,1,2,0:T(8,128)(2,1)}), bf16[32,64,1,128]{3,1,2,0:T(8,128)(2,1)S(1)}, u32[]{:S(2)}, u32[]{:S(2)}) async-start(bf16[32,64,1,128]{3,1,2,0:T(8,128)(2,1)} %broadcast_in_dim.86), calls=%async_computation.4 | async-start | bytes 1048576 | tf_op jit(solution)/shard_map/all_to_all | solution.py:16
  81.7 20.0 %all-to-all-start.2 = ((f32[64,1,128]{2,1,0:T(1,128)}), f32[64,1,128]{2,1,0:T(1,128)S(1)}, u32[]{:S(2)}, u32[]{:S(2)}) async-start(f32[64,1,128]{2,1,0:T(1,128)} %bitcast.13), calls=%async_computation.2 | async-start | bytes 65536 | tf_op jit(solution)/shard_map/all_to_all | solution.py:41
  103.1 6.0 %all-to-all-start.5 = ((bf16[2,32,64,1,128]{4,2,1,3,0:T(8,128)(2,1)}), bf16[2,32,64,1,128]{4,2,1,3,0:T(8,128)(2,1)S(1)}, u32[]{:S(2)}, u32[]{:S(2)}) async-start(bf16[2,32,64,1,128]{4,2,1,3,0:T(8,128)(2,1)} %broadcast_in_dim.88), calls=%async_computation.5 | async-start | bytes 2097152 | tf_op jit(solution)/shard_map/all_to_all | solution.py:16
  109.1 5.1 %copy-start = (bf16[2,32,64,1,128]{4,2,1,3,0:T(8,128)(2,1)}, bf16[2,32,64,1,128]{4,2,1,3,0:T(8,128)(2,1)S(1)}, u32[]{:S(2)}) copy-start(bf16[2,32,64,1,128]{4,2,1,3,0:T(8,128)(2,1)S(1)} %all-to-all-done.5) | copy-start | bytes 3145732
  109.7 13.9 %all-to-all-start.3 = ((f32[64,1,128]{2,1,0:T(1,128)}), f32[64,1,128]{2,1,0:T(1,128)S(1)}, u32[]{:S(2)}, u32[]{:S(2)}) async-start(f32[64,1,128]{2,1,0:T(1,128)} %broadcast_in_dim.84), calls=%async_computation.3 | async-start | bytes 65536 | tf_op jit(solution)/shard_map/all_to_all | solution.py:16
where the time goes:
time: 154 us; the launch traced here: 153 us
  waiting for transfers between devices  42 us (27%)
  local copies, waits for them, and re-layouts  37.9 us (25%)
  starting transfers between devices  36.3 us (24%)
  matrix products  20.9 us (14%)
  blocking collectives  8.74 us (6%)
  other arithmetic  6.36 us (4%)
    all_to_all x4, waiting for transfers between devices, copy_for_each(): lax.all_to_all(jnp.broadcast_to(shard[None], (devices, *shard.shape)), ax...  32.7 us
    all_to_all x4, starting transfers between devices, copy_for_each(): lax.all_to_all(jnp.broadcast_to(shard[None], (devices, *shard.shape)), ax...  25.7 us
    unnamed x8, local copies, waits for them, and re-layouts  12.1 us
    all_to_all x1, starting transfers between devices, sum_at_owner(): lax.all_to_all(tiles, axis, split_axis=0, concat_axis=0, tiled=True)  10.6 us
    dot_general x9, matrix products, row_scores(): lax.dot_general(query_rows, key_rows, (((1,), (1,)), ((), ())), preferred...  10.3 us
    reshape x1, local copies, waits for them, and re-layouts, per_device(): totals.astype(jnp.bfloat16).reshape(tok_count, group_size, totals.shape[1])  9.41 us
    all_to_all x1, waiting for transfers between devices, sum_at_owner(): lax.all_to_all(tiles, axis, split_axis=0, concat_axis=0, tiled=True)  9.31 us
    all_to_all x1, blocking collectives, copy_for_each(): lax.all_to_all(jnp.broadcast_to(shard[None], (devices, *shard.shape)), ax...  8.74 us
  transfers between devices with their start and end apart: 5, of which 4 were waited for; matrix products, arithmetic and copies ran while one was open for 20% of the time, Pallas kernels for 0%

commit v1 on v0

v1 whole, which is shorter than its diff:
```python
import functools
import math

import jax
import jax.numpy as jnp
from jax import lax
from jax.experimental import pallas as pl
from jax.experimental.pallas import tpu as pltpu
from jax.sharding import PartitionSpec as P

BLK = 128
WIN = 512
NX = 4
HEAD_CUT = 4
MESH = pl.DeviceIdType.MESH
VMEM = pltpu.VMEM


def refresh_kernel(
    nz, ws, q_hbm, k_hbm, b_hbm, bank_out, rep_out,
    qb, kb, bb, acc, pb, rb, rx,
    lsem, ksend, krecv, dsend, drecv, qsend, qrecv, bsend, brecv,
    cs, cr, es, er, ps, pr, xs, xr, osem,
):
    group, tok, hd = q_hbm.shape
    half_z = nz // 2
    groups = nz // 2
    s = lax.axis_index("seq")
    z, x, c = s // (2 * NX), (s // 2) % NX, s % 2
    xc = x * 2 + c
    exp_scale = math.log2(math.e) / math.sqrt(hd)

    def dev(zz, xx, cc):
        return {"seq": (lax.rem(zz, nz) * NX + lax.rem(xx, NX)) * 2 + cc}

    def remote(src, dst, ssem, rsem, target):
        return pltpu.make_async_remote_copy(
            src_ref=src, dst_ref=dst, send_sem=ssem, recv_sem=rsem,
            device_id=target, device_id_type=MESH,
        )

    sibling = dev(z, x, 1 - c)
    east, west = dev(z, x + 1, c), dev(z, x + NX - 1, c)

    own = [
        pltpu.make_async_copy(k_hbm, kb.at[0, 0], lsem.at[0]),
        pltpu.make_async_copy(q_hbm, qb.at[0], lsem.at[1]),
        pltpu.make_async_copy(b_hbm, bb.at[z, xc], lsem.at[2]),
    ]
    for copy in own:
        copy.start()

    peers = [dev(z + dz, x, (c + dc) % 2) for dz in range(nz) for dc in range(2) if dz or dc]
    peers += [dev(z, x + dx, (c + dc) % 2) for dx in range(1, NX) for dc in range(2)]
    barrier = pltpu.get_barrier_semaphore()
    for peer in peers:
        pl.semaphore_signal(barrier, inc=1, device_id=peer, device_id_type=MESH)
    acc[...] = jnp.zeros_like(acc)
    pl.semaphore_wait(barrier, len(peers))

    key_z = {d: remote(kb.at[0, 0], kb.at[d, 0], ksend.at[d], krecv.at[d], dev(z + d, x, c)) for d in range(1, nz)}
    key_core = {d: remote(kb.at[d, 0], kb.at[d, 1], dsend.at[d], drecv.at[d], sibling) for d in range(nz)}
    lo, hi = pl.ds(0, HEAD_CUT), pl.ds(HEAD_CUT, group - HEAD_CUT)

    def q_copy(i, src_slot, dst_slot, heads, target):
        return remote(qb.at[src_slot, heads], qb.at[dst_slot, heads], qsend.at[i], qrecv.at[i], target)

    q_x = [
        q_copy(0, 0, 1, lo, east), q_copy(1, 0, 1, hi, east),
        q_copy(2, 0, 3, hi, west), q_copy(3, 0, 3, lo, west),
        q_copy(4, 1, 2, lo, east), q_copy(5, 3, 2, hi, west),
    ]
    bank_z = {d: remote(bb.at[z, xc], bb.at[z, xc], bsend.at[d], brecv.at[d], dev(z + d, x, c)) for d in range(1, nz)}
    first, last = pl.ds(0, half_z), pl.ds(half_z, half_z)

    def c_copy(i, column, rows, target):
        return remote(bb.at[rows, column], bb.at[rows, column], cs.at[i], cr.at[i], target)

    def column(dx):
        return lax.rem(x + dx, NX) * 2 + c

    west_of, east_of = column(NX - 1), column(1)
    bank_x = [
        c_copy(0, xc, first, east), c_copy(1, xc, last, east),
        c_copy(2, xc, last, west), c_copy(3, xc, first, west),
        c_copy(4, west_of, first, east), c_copy(5, east_of, last, west),
    ]
    bank_in = [
        c_copy(0, west_of, first, east), c_copy(1, west_of, last, east),
        c_copy(2, east_of, last, west), c_copy(3, east_of, first, west),
        c_copy(4, column(2), first, east), c_copy(5, column(2), last, west),
    ]

    def e_copy(dx):
        return remote(bb.at[:, column(dx)], bb.at[:, column(dx)], es.at[dx], er.at[dx], sibling)

    bank_core = [e_copy(dx) for dx in range(NX)]

    def start_all():
        own[0].wait()
        key_core[0].start()
        order = sorted(range(1, nz), key=lambda d: (min(d, nz - d), d))
        for d in order:
            key_z[d].start()
        own[1].wait()
        for i in (0, 2, 1, 3):
            q_x[i].start()
        own[2].wait()
        for d in order:
            bank_z[d].start()

    def forward_key(*offsets):
        for d in offsets:
            key_z[d].wait_recv()
            key_core[d].start()

    def have_keys(*offsets):
        for d in offsets:
            key_core[d].wait_recv()

    def forward_queries():
        q_x[0].wait_recv()
        q_x[4].start()
        q_x[2].wait_recv()
        q_x[5].start()

    def bank_rows():
        for d in range(1, nz):
            bank_z[d].wait_recv()
        for i in (0, 2, 1, 3):
            bank_x[i].start()
        bank_core[0].start()

    def bank_forward():
        bank_in[0].wait_recv()
        bank_x[4].start()
        bank_in[2].wait_recv()
        bank_x[5].start()

    def bank_cross():
        bank_in[1].wait_recv()
        bank_core[3].start()
        bank_in[3].wait_recv()
        bank_core[1].start()

    def at_step(step):
        tile, g = step // groups, step % groups
        if step == 0:
            start_all()
        if tile == 0:
            near = [d for d in {g + 1, (nz - g) % nz} if d]
            forward_key(*near)
            if g == min(1, groups - 1):
                forward_queries()
            have_keys(*sorted({g + 1, (nz - g) % nz}))
        if tile == 1 and g == 0:
            q_x[1].wait_recv()
            bank_rows()
        if tile == 2 and g == 0:
            q_x[3].wait_recv()
        if tile == 2 and g == groups - 1:
            bank_forward()
        if tile == 3 and g == 0:
            q_x[4].wait_recv()
            q_x[5].wait_recv()

    lane = lax.broadcasted_iota(jnp.int32, (1, BLK), 1)

    def compute(step):
        tile, g = step // groups, step % groups
        slot = tile ^ (tile >> 1)
        base = (z * 2 * NX + lax.rem(x - slot + NX, NX) * 2 + c) * tok
        position = base + lane
        offsets = [lax.rem(nz - g, nz), g + 1]
        members = [(d, rel) for d in offsets for rel in range(2)]
        keys = jnp.concatenate([kb[d].reshape(2 * BLK, hd) for d in offsets], axis=0)
        inside = []
        for d, rel in members:
            block = (lax.rem(z - d + nz, nz) * NX + x) * 2 + (c + rel) % 2
            begin = ws[block]
            inside.append(((position >= begin) & (position < begin + WIN)).astype(jnp.float32))
        sums = [acc[d, rel] for d, rel in members]
        for h in range(0, group, 2):
            heads = min(2, group - h)
            rows = qb[slot, pl.ds(h, heads)].reshape(heads * tok, hd)
            scores = lax.dot_general(
                keys, rows, (((1,), (1,)), ((), ())), preferred_element_type=jnp.float32
            )
            for i in range(len(members)):
                part = scores[i * BLK : (i + 1) * BLK]
                top = jnp.max(part, axis=0, keepdims=True)
                e = jnp.exp2((part - top) * exp_scale)
                total = jnp.sum(e, axis=0, keepdims=True)
                for j in range(heads):
                    cut = slice(j * tok, (j + 1) * tok)
                    sums[i] = sums[i] + e[:, cut] * (inside[i] / total[:, cut])
        for (d, rel), value in zip(members, sums):
            acc[d, rel] = value

    @pl.loop(0, NX * groups)
    def _(step):
        for k in range(NX * groups):
            pl.when(step == k)(functools.partial(at_step, k))
        compute(step)

    for d in range(nz):
        for rel in range(2):
            weight = jnp.sum(acc[d, rel], axis=1, keepdims=True)
            row = jnp.sum(weight * kb[d, rel].astype(jnp.float32), axis=0, keepdims=True)
            pb[(c + rel) % 2, pl.ds(lax.rem(z - d + nz, nz), 1), :] = row

    column_peers = [(dz, dc) for dz in range(nz) for dc in range(2) if dz or dc]
    parts = [
        remote(pb.at[(c + dc) % 2], rb.at[dz * 2 + dc], ps.at[dz * 2 + dc], pr.at[dz * 2 + dc], dev(z + dz, x, (c + dc) % 2))
        for dz, dc in column_peers
    ]
    for copy in parts:
        copy.start()
    rb[0] = pb[c]
    bank_cross()
    for copy in parts:
        copy.wait_recv()
    total = jnp.zeros((nz, hd), jnp.float32)
    for dz in range(nz):
        for dc in range(2):
            total = total + rb[lax.rem(z - dz + nz, nz) * 2 + (c + dc) % 2]
    mine = pl.ds(pl.multiple_of(xc * nz, nz), nz)
    rx[mine, :] = total / (group * WIN)
    row_peers = [(dx, dc) for dx in range(NX) for dc in range(2) if dx or dc]
    sums_x = [
        remote(rx.at[mine], rx.at[mine], xs.at[dx * 2 + dc], xr.at[dx * 2 + dc], dev(z, x + dx, (c + dc) % 2))
        for dx, dc in row_peers
    ]
    for copy in sums_x:
        copy.start()
    bank_in[4].wait_recv()
    bank_in[5].wait_recv()
    bank_core[2].start()
    for copy in bank_core:
        copy.wait_recv()
    bank_done = pltpu.make_async_copy(bb, bank_out, osem.at[0])
    bank_done.start()
    for copy in sums_x:
        copy.wait_recv()
    for zz in range(0, nz, 2):
        pair = [rx[pl.ds(zz + i, 2 * NX, stride=nz), :] for i in range(2)]
        rep_out[pl.ds(zz * 2 * NX, 4 * NX), :] = jnp.concatenate(pair, axis=0).astype(jnp.bfloat16)
    for copy in [*key_z.values(), *key_core.values(), *q_x, *bank_z.values(), *bank_x, *bank_core, *parts, *sums_x]:
        copy.wait_send()
    bank_done.wait()


def refresh(nz, window_start, q, k, b):
    group, tok, hd = q.shape
    hbm = pl.BlockSpec(memory_space=pl.ANY)
    dma = pltpu.SemaphoreType.DMA
    bank_shape = (nz, 2 * NX, *b.shape)
    return pl.pallas_call(
        functools.partial(refresh_kernel, nz),
        out_shape=(
            jax.ShapeDtypeStruct(bank_shape, jnp.bfloat16),
            jax.ShapeDtypeStruct((nz * 2 * NX, hd), jnp.bfloat16),
        ),
        in_specs=[pl.BlockSpec(memory_space=pltpu.SMEM), hbm, hbm, hbm],
        out_specs=(hbm, pl.BlockSpec(memory_space=VMEM)),
        scratch_shapes=[
            VMEM((NX, group, tok, hd), jnp.bfloat16),
            VMEM((nz, 2, BLK, hd), jnp.bfloat16),
            VMEM(bank_shape, jnp.bfloat16),
            VMEM((nz, 2, BLK, BLK), jnp.float32),
            VMEM((2, nz, hd), jnp.float32),
            VMEM((2 * nz, nz, hd), jnp.float32),
            VMEM((2 * NX * nz, hd), jnp.float32),
            dma((3,)),
            dma((nz,)), dma((nz,)), dma((nz,)), dma((nz,)),
            dma((6,)), dma((6,)),
            dma((nz,)), dma((nz,)),
            dma((6,)), dma((6,)), dma((NX,)), dma((NX,)),
            dma((2 * nz,)), dma((2 * nz,)), dma((2 * NX,)), dma((2 * NX,)),
            dma((1,)),
        ],
        compiler_params=pltpu.CompilerParams(collective_id=0, has_side_effects=True),
        name="refresh",
    )(window_start, q, k, b)


def patched(slots, first_row, reps, rows):
    count = rows.shape[0]
    row = first_row + lax.broadcasted_iota(jnp.int32, (count, slots.shape[1]), 0)
    chosen = (row == slots).astype(jnp.bfloat16)
    both = jnp.concatenate([reps, jnp.ones_like(reps)], axis=1)
    placed = jnp.dot(chosen, both, preferred_element_type=jnp.float32)
    hd = reps.shape[1]
    return jnp.where(placed[:, hd:] > 0.5, placed[:, :hd], rows.astype(jnp.float32)).astype(jnp.bfloat16)


def relevance_kernel(slots, q, bank, reps, shard, out, shard_out):
    step = pl.program_id(0)
    width = bank.shape[0]
    tile = patched(slots[...], step * width, reps[...], bank[...])
    scores = lax.dot_general(q[...], tile, (((1,), (1,)), ((), ())), preferred_element_type=jnp.float32)
    out[...] = (scores * (1.0 / math.sqrt(q.shape[1]))).astype(jnp.bfloat16)

    @pl.when(step == 0)
    def _():
        first_row = lax.axis_index("seq") * shard.shape[0]
        shard_out[...] = patched(slots[...], first_row, reps[...], shard[...])


def relevance_of(slots, q, bank, reps, shard, tile=512):
    rows, hd = q.shape
    total = bank.shape[0]

    def whole(array):
        return pl.BlockSpec(array.shape, lambda i: (0, 0))

    return pl.pallas_call(
        relevance_kernel,
        grid=(total // tile,),
        out_shape=(
            jax.ShapeDtypeStruct((rows, total), jnp.bfloat16),
            jax.ShapeDtypeStruct(shard.shape, jnp.bfloat16),
        ),
        in_specs=[whole(slots), whole(q), pl.BlockSpec((tile, hd), lambda i: (i, 0)), whole(reps), whole(shard)],
        out_specs=(pl.BlockSpec((rows, tile), lambda i: (0, i)), whole(shard)),
        compiler_params=pltpu.CompilerParams(dimension_semantics=("arbitrary",)),
        name="relevance",
    )(slots, q, bank, reps, shard)


def per_device(nz, queries, new_keys, cache_keys, window_start, owner_slot):
    tok, group, hd = queries.shape
    q = queries.transpose(1, 0, 2)
    shard = cache_keys[:, 0, :]
    bank, reps = refresh(nz, window_start, q, new_keys[:, 0, :], shard)
    total = nz * 2 * NX * shard.shape[0]
    relevance, new_shard = relevance_of(
        owner_slot.reshape(1, -1), q.reshape(group * tok, hd), bank.reshape(total, hd), reps, shard
    )
    relevance = relevance.reshape(group, tok, total).transpose(1, 0, 2)
    return (relevance, new_shard[:, None, :])


def solution(mesh):
    nz = mesh.shape["seq"] // (2 * NX)
    split = P("seq", "kvh", None)
    return jax.shard_map(
        functools.partial(per_device, nz),
        mesh=mesh,
        in_specs=(split, split, split, P(), P()),
        out_specs=(split, split),
        check_vma=False,
    )
```

time: 154 us -> 53.9 us (0.35)
  Pallas kernels: 0 us -> 53 us
  waiting for transfers between devices: 42 us -> 0 us
  local copies, waits for them, and re-layouts: 37.9 us -> 0 us
  starting transfers between devices: 36.3 us -> 0 us
  matrix products: 20.9 us -> 0 us
  blocking collectives: 8.74 us -> 0 us
  other arithmetic: 6.36 us -> 0 us
    pallas_call x0 -> x2, Pallas kernels: none -> 53 us  [the longest x1 44.5 us: refresh(): pl.pallas_call(functools.partial(refresh_kernel, nz), out_shape=(jax.Shap...]
    all_to_all x5 -> x0, waiting for transfers between devices: 42 us -> none  [the longest x4 32.7 us: copy_for_each(): lax.all_to_all(jnp.broadcast_to(shard[None], (devices, *shard.shape)), ax...]
    all_to_all x5 -> x0, starting transfers between devices: 36.3 us -> none  [the longest x4 25.7 us: copy_for_each(): lax.all_to_all(jnp.broadcast_to(shard[None], (devices, *shard.shape)), ax...]
    dot_general x20 -> x0, matrix products: 20.9 us -> none  [the longest x9 10.3 us: row_scores(): lax.dot_general(query_rows, key_rows, (((1,), (1,)), ((), ())), preferred...]
    unnamed x8 -> x0, local copies, waits for them, and re-layouts: 12.1 us -> none
    reshape x2 -> x0, local copies, waits for them, and re-layouts: 9.49 us -> none  [the longest x1 9.41 us: per_device(): totals.astype(jnp.bfloat16).reshape(tok_count, group_size, totals.shape[1])]
    all_to_all x1 -> x0, blocking collectives: 8.74 us -> none  [copy_for_each(): lax.all_to_all(jnp.broadcast_to(shard[None], (devices, *shard.shape)), ax...]
    reduce_sum x11 -> x0, other arithmetic: 5.58 us -> none  [the longest x8 5.2 us: group_sums(): softmax_weights = jax.nn.softmax(scores, axis=-1)]
  transfers between devices with their start and end apart: 5 -> 0, of which waited for: 4 -> 0; matrix products, arithmetic and copies ran while one was open for 20% -> 0% of each run, Pallas kernels for 0% -> 0%
where the time goes in v1:
time: 53.9 us; the launch traced here: 53.6 us
  Pallas kernels  53 us (98%)
  between operations  0.64 us (1%)
    pallas_call x1, Pallas kernels, refresh(): pl.pallas_call(functools.partial(refresh_kernel, nz), out_shape=(jax.Shap...  44.5 us
    pallas_call x1, Pallas kernels, relevance_of(): pl.pallas_call(relevance_kernel, grid=(total // tile,), out_shape=(jax.Sh...  8.53 us

profile of v1, /device:TPU:1, one launch (start us, length us, event | category | flops | bytes accessed | tf_op | source)
XLA Modules:
  0.0 53.6 jit_solution(9622005605859954328)
XLA Ops:
  0.6 44.5 %refresh.1 = (bf16[8,8,64,128]{3,2,1,0:T(8,128)(2,1)}, bf16[64,128]{1,0:T(8,128)(2,1)}) custom-call(s32[64]{0:T(128)} %ws.1, bf16[7,128,128]{2,1,0:T(8,128)(2,1)} %bitcast.12, bf16[128,128]{1,0:T(8,128)(2,1)} %bitcast.16, bf16[64,128]{1,0:T(8,128)(2,1)} %bitcast.14), custom_call_target="tpu_custom_call" | custom-call | tf_op jit(solution)/shard_map/refresh/pallas_call | solution.py:258
  45.1 8.5 %relevance.1 = (bf16[896,4096]{1,0:T(8,128)(2,1)}, bf16[64,128]{1,0:T(8,128)(2,1)}) custom-call(s32[1,64]{1,0:T(1,128)} %bitcast.17, bf16[896,128]{1,0:T(8,128)(2,1)} %bitcast.13, bf16[4096,128]{1,0:T(8,128)(2,1)} %bitcast.11, bf16[64,128]{1,0:T(8,128)(2,1)} %get-tuple-element.7.reps, bf16[64,128]{1,0:T(8,128)(2,1)} %bitcast.15), custom_call_target="tpu_custom_call" | custom-call | tf_op jit(solution)/shard_map/relevance/pallas_call | solution.py:317

commit v2 on v1

--- a/solution.py
+++ b/solution.py
@@ -16,15 +16,24 @@
 VMEM = pltpu.VMEM
 
 
+def on_chip(shape, dtype):
+    return VMEM(shape, dtype)
+
+
+def kept(array):
+    return pltpu.with_memory_space_constraint(array, VMEM)
+
+
 def refresh_kernel(
-    nz, ws, q_hbm, k_hbm, b_hbm, bank_out, rep_out,
+    nz, ws, slots, q_hbm, k_hbm, b_hbm, rhs_out, lhs_out, shard_out,
     qb, kb, bb, acc, pb, rb, rx,
     lsem, ksend, krecv, dsend, drecv, qsend, qrecv, bsend, brecv,
-    cs, cr, es, er, ps, pr, xs, xr, osem,
+    cs, cr, es, er, ps, pr, xs, xr,
 ):
     group, tok, hd = q_hbm.shape
     half_z = nz // 2
-    groups = nz // 2
+    per = min(4, nz)
+    groups = nz // per
     s = lax.axis_index("seq")
     z, x, c = s // (2 * NX), (s // 2) % NX, s % 2
     xc = x * 2 + c
@@ -96,25 +105,25 @@
 
     bank_core = [e_copy(dx) for dx in range(NX)]
 
+    near = [0, 1, nz - 1, 2][:per]
+
     def start_all():
         own[0].wait()
         key_core[0].start()
-        order = sorted(range(1, nz), key=lambda d: (min(d, nz - d), d))
-        for d in order:
+        for d in sorted(range(1, nz), key=lambda d: (min(d, nz - d), d)):
             key_z[d].start()
         own[1].wait()
         for i in (0, 2, 1, 3):
             q_x[i].start()
-        own[2].wait()
-        for d in order:
-            bank_z[d].start()
+        lhs_out[:, :hd] = qb[0].reshape(group * tok, hd)
 
     def forward_key(*offsets):
         for d in offsets:
-            key_z[d].wait_recv()
-            key_core[d].start()
-
-    def have_keys(*offsets):
+            if d in key_z:
+                key_z[d].wait_recv()
+                key_core[d].start()
+
+    def have_keys(offsets):
         for d in offsets:
             key_core[d].wait_recv()
 
@@ -144,62 +153,62 @@
         bank_core[1].start()
 
     def at_step(step):
-        tile, g = step // groups, step % groups
+        pair, g = step // groups, step % groups
         if step == 0:
             start_all()
-        if tile == 0:
-            near = [d for d in {g + 1, (nz - g) % nz} if d]
-            forward_key(*near)
-            if g == min(1, groups - 1):
-                forward_queries()
-            have_keys(*sorted({g + 1, (nz - g) % nz}))
-        if tile == 1 and g == 0:
+            forward_key(1)
+            if nz > 2:
+                forward_key(nz - 1, 2)
+            forward_queries()
+            own[2].wait()
+            for d in range(1, nz):
+                bank_z[d].start()
+            if nz > 4:
+                forward_key(nz - 2)
+            have_keys(near)
             q_x[1].wait_recv()
+            q_x[3].wait_recv()
+        if pair == 0 and g == 1:
+            forward_key(3, nz - 3, 4)
+            have_keys([d for d in range(nz) if d not in near])
+        if pair == 1 and g == 0:
             bank_rows()
-        if tile == 2 and g == 0:
-            q_x[3].wait_recv()
-        if tile == 2 and g == groups - 1:
-            bank_forward()
-        if tile == 3 and g == 0:
             q_x[4].wait_recv()
             q_x[5].wait_recv()
 
     lane = lax.broadcasted_iota(jnp.int32, (1, BLK), 1)
 
     def compute(step):
-        tile, g = step // groups, step % groups
-        slot = tile ^ (tile >> 1)
-        base = (z * 2 * NX + lax.rem(x - slot + NX, NX) * 2 + c) * tok
-        position = base + lane
-        offsets = [lax.rem(nz - g, nz), g + 1]
+        pair, g = step // groups, step % groups
+        tiles = (1 - pair, 3 - pair)
+        offsets = near if groups == 1 else [6 * g, 1 + 2 * g, 7 - 2 * g, 2 + 2 * g]
         members = [(d, rel) for d in offsets for rel in range(2)]
         keys = jnp.concatenate([kb[d].reshape(2 * BLK, hd) for d in offsets], axis=0)
-        inside = []
+        position = [(z * 2 * NX + lax.rem(x - t + NX, NX) * 2 + c) * tok + lane for t in tiles]
+        first_in, any_in = [], []
         for d, rel in members:
-            block = (lax.rem(z - d + nz, nz) * NX + x) * 2 + (c + rel) % 2
-            begin = ws[block]
-            inside.append(((position >= begin) & (position < begin + WIN)).astype(jnp.float32))
+            begin = ws[(lax.rem(z - d + nz, nz) * NX + x) * 2 + (c + rel) % 2]
+            hit = [(p >= begin) & (p < begin + WIN) for p in position]
+            first_in.append(hit[0])
+            any_in.append((hit[0] | hit[1]).astype(jnp.float32))
         sums = [acc[d, rel] for d, rel in members]
-        for h in range(0, group, 2):
-            heads = min(2, group - h)
-            rows = qb[slot, pl.ds(h, heads)].reshape(heads * tok, hd)
+        for h in range(group):
+            rows = jnp.concatenate([qb[t, h] for t in tiles], axis=0)
             scores = lax.dot_general(
                 keys, rows, (((1,), (1,)), ((), ())), preferred_element_type=jnp.float32
             )
             for i in range(len(members)):
-                part = scores[i * BLK : (i + 1) * BLK]
+                both = scores[i * BLK : (i + 1) * BLK]
+                part = jnp.where(first_in[i], both[:, :tok], both[:, tok:])
                 top = jnp.max(part, axis=0, keepdims=True)
                 e = jnp.exp2((part - top) * exp_scale)
-                total = jnp.sum(e, axis=0, keepdims=True)
-                for j in range(heads):
-                    cut = slice(j * tok, (j + 1) * tok)
-                    sums[i] = sums[i] + e[:, cut] * (inside[i] / total[:, cut])
+                sums[i] = sums[i] + e * (any_in[i] / jnp.sum(e, axis=0, keepdims=True))
         for (d, rel), value in zip(members, sums):
             acc[d, rel] = value
 
-    @pl.loop(0, NX * groups)
+    @pl.loop(0, 2 * groups)
     def _(step):
-        for k in range(NX * groups):
+        for k in range(2 * groups):
             pl.when(step == k)(functools.partial(at_step, k))
         compute(step)
 
@@ -217,6 +226,7 @@
     for copy in parts:
         copy.start()
     rb[0] = pb[c]
+    bank_forward()
     bank_cross()
     for copy in parts:
         copy.wait_recv()
@@ -238,31 +248,56 @@
     bank_core[2].start()
     for copy in bank_core:
         copy.wait_recv()
-    bank_done = pltpu.make_async_copy(bb, bank_out, osem.at[0])
-    bank_done.start()
+    columns = jnp.concatenate([slots[...], slots[...]], axis=1)
+    width = 2 * NX * b_hbm.shape[0]
+
+    def hits(first_row, count):
+        row = first_row + lax.broadcasted_iota(jnp.int32, (count, columns.shape[1]), 0)
+        chosen = (row == columns).astype(jnp.float32)
+        return chosen, jnp.max(chosen, axis=1, keepdims=True) > 0.5
+
+    @pl.loop(0, nz)
+    def _(zz):
+        start = pl.multiple_of(zz * width, width)
+        chosen, taken = hits(start, width)
+        rest = jnp.where(taken, 0.0, bb[zz].reshape(width, hd).astype(jnp.float32))
+        rhs_out[pl.ds(start, width), :] = jnp.concatenate([rest, chosen], axis=1).astype(jnp.bfloat16)
+
     for copy in sums_x:
         copy.wait_recv()
-    for zz in range(0, nz, 2):
-        pair = [rx[pl.ds(zz + i, 2 * NX, stride=nz), :] for i in range(2)]
-        rep_out[pl.ds(zz * 2 * NX, 4 * NX), :] = jnp.concatenate(pair, axis=0).astype(jnp.bfloat16)
+    ordered = [rx[pl.ds(zz, 2 * NX, stride=nz), :] for zz in range(nz)]
+    reps = jnp.concatenate(ordered, axis=0).astype(jnp.bfloat16)
+    value = lax.dot_general(
+        lhs_out[:, :hd], reps, (((1,), (1,)), ((), ())), preferred_element_type=jnp.float32
+    )
+    high = value.astype(jnp.bfloat16)
+    low = (value - high.astype(jnp.float32)).astype(jnp.bfloat16)
+    lhs_out[:, hd:] = jnp.concatenate([high, low], axis=1)
+    held = b_hbm.shape[0]
+    chosen, taken = hits(s * held, held)
+    placed = jnp.dot(
+        chosen[:, : reps.shape[0]].astype(jnp.bfloat16), reps, preferred_element_type=jnp.float32
+    )
+    shard_out[...] = jnp.where(taken, placed, bb[z, xc].astype(jnp.float32)).astype(jnp.bfloat16)
     for copy in [*key_z.values(), *key_core.values(), *q_x, *bank_z.values(), *bank_x, *bank_core, *parts, *sums_x]:
         copy.wait_send()
-    bank_done.wait()
-
-
-def refresh(nz, window_start, q, k, b):
+
+
+def refresh(nz, window_start, slots, q, k, b):
     group, tok, hd = q.shape
     hbm = pl.BlockSpec(memory_space=pl.ANY)
+    vmem = pl.BlockSpec(memory_space=VMEM)
     dma = pltpu.SemaphoreType.DMA
     bank_shape = (nz, 2 * NX, *b.shape)
     return pl.pallas_call(
         functools.partial(refresh_kernel, nz),
         out_shape=(
-            jax.ShapeDtypeStruct(bank_shape, jnp.bfloat16),
-            jax.ShapeDtypeStruct((nz * 2 * NX, hd), jnp.bfloat16),
+            on_chip((nz * 2 * NX * b.shape[0], hd + 2 * slots.shape[1]), jnp.bfloat16),
+            on_chip((group * tok, hd + 2 * slots.shape[1]), jnp.bfloat16),
+            on_chip(b.shape, jnp.bfloat16),
         ),
-        in_specs=[pl.BlockSpec(memory_space=pltpu.SMEM), hbm, hbm, hbm],
-        out_specs=(hbm, pl.BlockSpec(memory_space=VMEM)),
+        in_specs=[pl.BlockSpec(memory_space=pltpu.SMEM), vmem, hbm, hbm, hbm],
+        out_specs=(vmem, vmem, vmem),
         scratch_shapes=[
             VMEM((NX, group, tok, hd), jnp.bfloat16),
             VMEM((nz, 2, BLK, hd), jnp.bfloat16),
@@ -277,67 +312,58 @@
             dma((nz,)), dma((nz,)),
             dma((6,)), dma((6,)), dma((NX,)), dma((NX,)),
             dma((2 * nz,)), dma((2 * nz,)), dma((2 * NX,)), dma((2 * NX,)),
-            dma((1,)),
         ],
         compiler_params=pltpu.CompilerParams(collective_id=0, has_side_effects=True),
         name="refresh",
-    )(window_start, q, k, b)
-
-
-def patched(slots, first_row, reps, rows):
-    count = rows.shape[0]
-    row = first_row + lax.broadcasted_iota(jnp.int32, (count, slots.shape[1]), 0)
-    chosen = (row == slots).astype(jnp.bfloat16)
-    both = jnp.concatenate([reps, jnp.ones_like(reps)], axis=1)
-    placed = jnp.dot(chosen, both, preferred_element_type=jnp.float32)
-    hd = reps.shape[1]
-    return jnp.where(placed[:, hd:] > 0.5, placed[:, :hd], rows.astype(jnp.float32)).astype(jnp.bfloat16)
-
-
-def relevance_kernel(slots, q, bank, reps, shard, out, shard_out):
-    step = pl.program_id(0)
-    width = bank.shape[0]
-    tile = patched(slots[...], step * width, reps[...], bank[...])
-    scores = lax.dot_general(q[...], tile, (((1,), (1,)), ((), ())), preferred_element_type=jnp.float32)
-    out[...] = (scores * (1.0 / math.sqrt(q.shape[1]))).astype(jnp.bfloat16)
-
-    @pl.when(step == 0)
-    def _():
-        first_row = lax.axis_index("seq") * shard.shape[0]
-        shard_out[...] = patched(slots[...], first_row, reps[...], shard[...])
-
-
-def relevance_of(slots, q, bank, reps, shard, tile=512):
-    rows, hd = q.shape
-    total = bank.shape[0]
-
-    def whole(array):
-        return pl.BlockSpec(array.shape, lambda i: (0, 0))
-
+    )(window_start, slots, q, k, b)
+
+
+def relevance_kernel(tile, lhs, rhs, shard, out, shard_out, held, sem):
+    scale = 1.0 / math.sqrt(BLK)
+    copies = [pltpu.make_async_copy(shard, shard_out, sem.at[0])]
+    copies[0].start()
+    for i in range(out.shape[1] // tile):
+        cut = pl.ds(i * tile, tile)
+        scores = lax.dot_general(
+            lhs[...], rhs[cut, :], (((1,), (1,)), ((), ())), preferred_element_type=jnp.float32
+        )
+        held[:, cut] = (scores * scale).astype(jnp.bfloat16)
+        copy = pltpu.make_async_copy(held.at[:, cut], out.at[:, cut], sem.at[i + 1])
+        copy.start()
+        copies.append(copy)
+    for copy in copies:
+        copy.wait()
+
+
+def relevance_of(lhs, rhs, shard, tile=512):
+    rows, total = lhs.shape[0], rhs.shape[0]
+    vmem = pl.BlockSpec(memory_space=VMEM)
+    hbm = pl.BlockSpec(memory_space=pl.ANY)
+    lhs, rhs, shard = (kept(a) for a in (lhs, rhs, shard))
     return pl.pallas_call(
-        relevance_kernel,
-        grid=(total // tile,),
+        functools.partial(relevance_kernel, tile),
         out_shape=(
             jax.ShapeDtypeStruct((rows, total), jnp.bfloat16),
             jax.ShapeDtypeStruct(shard.shape, jnp.bfloat16),
         ),
-        in_specs=[whole(slots), whole(q), pl.BlockSpec((tile, hd), lambda i: (i, 0)), whole(reps), whole(shard)],
-        out_specs=(pl.BlockSpec((rows, tile), lambda i: (0, i)), whole(shard)),
-        compiler_params=pltpu.CompilerParams(dimension_semantics=("arbitrary",)),
+        in_specs=[vmem, vmem, vmem],
+        out_specs=(hbm, hbm),
+        scratch_shapes=[
+            VMEM((rows, total), jnp.bfloat16),
+            pltpu.SemaphoreType.DMA((1 + total // tile,)),
+        ],
         name="relevance",
-    )(slots, q, bank, reps, shard)
+    )(lhs, rhs, shard)
 
 
 def per_device(nz, queries, new_keys, cache_keys, window_start, owner_slot):
     tok, group, hd = queries.shape
     q = queries.transpose(1, 0, 2)
-    shard = cache_keys[:, 0, :]
-    bank, reps = refresh(nz, window_start, q, new_keys[:, 0, :], shard)
-    total = nz * 2 * NX * shard.shape[0]
-    relevance, new_shard = relevance_of(
-        owner_slot.reshape(1, -1), q.reshape(group * tok, hd), bank.reshape(total, hd), reps, shard
+    rhs, lhs, shard = refresh(
+        nz, window_start, owner_slot.reshape(1, -1), q, new_keys[:, 0, :], cache_keys[:, 0, :]
     )
-    relevance = relevance.reshape(group, tok, total).transpose(1, 0, 2)
+    relevance, new_shard = relevance_of(lhs, rhs, shard)
+    relevance = relevance.reshape(group, tok, rhs.shape[0]).transpose(1, 0, 2)
     return (relevance, new_shard[:, None, :])
 
 

time: 53.9 us -> 41.6 us (0.77)
  Pallas kernels: 53 us -> 40.9 us
    pallas_call x2, Pallas kernels: 53 us -> 40.9 us  [the longest x1 37.4 us: refresh(): pl.pallas_call(functools.partial(refresh_kernel, nz), out_shape=(on_chip(...]
where the time goes in v2:
time: 41.6 us; the launch traced here: 41.5 us
  Pallas kernels  40.9 us (98%)
  between operations  0.64 us (2%)
    pallas_call x1, Pallas kernels, refresh(): pl.pallas_call(functools.partial(refresh_kernel, nz), out_shape=(on_chip(...  37.4 us
    pallas_call x1, Pallas kernels, relevance_of(): pl.pallas_call(functools.partial(relevance_kernel, tile), out_shape=(jax....  3.5 us

profile of v2, /device:TPU:1, one launch (start us, length us, event | category | flops | bytes accessed | tf_op | source)
XLA Modules:
  0.0 41.5 jit_solution(4102421565116740174)
XLA Ops:
  0.6 37.4 %refresh.1 = (bf16[4096,256]{1,0:T(8,128)(2,1)S(1)}, bf16[896,256]{1,0:T(8,128)(2,1)S(1)}, bf16[64,128]{1,0:T(8,128)(2,1)S(1)}) custom-call(s32[64]{0:T(128)} %ws.1, s32[1,64]{1,0:T(1,128)} %bitcast.11, bf16[7,128,128]{2,1,0:T(8,128)(2,1)} %bitcast.8, bf16[128,128]{1,0:T(8,128)(2,1)} %bitcast.9, bf16[64,128]{1,0:T(8,128)(2,1)} %bitcast.10), custom_call_target="tpu_custom_call" | custom-call | tf_op jit(solution)/shard_map/refresh/pallas_call | solution.py:292
  38.0 3.5 %relevance.1 = (bf16[896,4096]{1,0:T(8,128)(2,1)}, bf16[64,128]{1,0:T(8,128)(2,1)}) custom-call(bf16[896,256]{1,0:T(8,128)(2,1)S(1)} %get-tuple-element.7.lhs, bf16[4096,256]{1,0:T(8,128)(2,1)S(1)} %get-tuple-element.8.rhs, bf16[64,128]{1,0:T(8,128)(2,1)S(1)} %get-tuple-element.9.shard), custom_call_target="tpu_custom_call" | custom-call | tf_op jit(solution)/shard_map/relevance/pallas_call | solution.py:343

commit v3 on v2

--- a/solution.py
+++ b/solution.py
@@ -25,12 +25,13 @@
 
 
 def refresh_kernel(
-    nz, ws, slots, q_hbm, k_hbm, b_hbm, rhs_out, lhs_out, shard_out,
-    qb, kb, bb, acc, pb, rb, rx,
+    nz, ws_hbm, slots_hbm, q_hbm, k_hbm, b_hbm, rhs_out, lhs_out, shard_out,
+    ws, slots, qb, kb, bb, keep, acc, pb, rb, rx,
     lsem, ksend, krecv, dsend, drecv, qsend, qrecv, bsend, brecv,
     cs, cr, es, er, ps, pr, xs, xr,
 ):
     group, tok, hd = q_hbm.shape
+    held = b_hbm.shape[0]
     half_z = nz // 2
     per = min(4, nz)
     groups = nz // per
@@ -55,19 +56,64 @@
         pltpu.make_async_copy(k_hbm, kb.at[0, 0], lsem.at[0]),
         pltpu.make_async_copy(q_hbm, qb.at[0], lsem.at[1]),
         pltpu.make_async_copy(b_hbm, bb.at[z, xc], lsem.at[2]),
+        pltpu.make_async_copy(slots_hbm, slots, lsem.at[3]),
+        pltpu.make_async_copy(ws_hbm, ws, lsem.at[4]),
     ]
     for copy in own:
         copy.start()
 
-    peers = [dev(z + dz, x, (c + dc) % 2) for dz in range(nz) for dc in range(2) if dz or dc]
-    peers += [dev(z, x + dx, (c + dc) % 2) for dx in range(1, NX) for dc in range(2)]
+    direct = sorted({d % nz for d in (1, -1, 2, -2)} - {0}, key=lambda d: (min(d, nz - d), d))
+    peers = [sibling, east, west] + [dev(z + d, x, c) for d in direct]
     barrier = pltpu.get_barrier_semaphore()
     for peer in peers:
         pl.semaphore_signal(barrier, inc=1, device_id=peer, device_id_type=MESH)
-    acc[...] = jnp.zeros_like(acc)
+
     pl.semaphore_wait(barrier, len(peers))
 
-    key_z = {d: remote(kb.at[0, 0], kb.at[d, 0], ksend.at[d], krecv.at[d], dev(z + d, x, c)) for d in range(1, nz)}
+    width = 2 * NX * held
+
+    def hits(first_row, count):
+        columns = jnp.concatenate([slots[...], slots[...]], axis=1)
+        row = first_row + lax.broadcasted_iota(jnp.int32, (count, columns.shape[1]), 0)
+        chosen = (row == columns).astype(jnp.float32)
+        return chosen, jnp.max(chosen, axis=1, keepdims=True)
+
+    def prepare():
+        acc[...] = jnp.zeros_like(acc)
+        own[3].wait()
+
+        @pl.loop(0, nz)
+        def _(zz):
+            start = pl.ds(pl.multiple_of(zz * width, width), width)
+            chosen, taken = hits(zz * width, width)
+            rhs_out[start, hd:] = chosen.astype(jnp.bfloat16)
+            keep[start, :] = jnp.broadcast_to(1.0 - taken, (width, hd)).astype(jnp.bfloat16)
+
+        lhs_out[:, :hd] = qb[0].reshape(group * tok, hd)
+
+    def k_copy(i, source, target, rows, to):
+        return remote(kb.at[source, 0, rows], kb.at[target, 0, rows], ksend.at[i], krecv.at[i], to)
+
+    def b_copy(i, dz, rows, to):
+        ref = bb.at[lax.rem(z + dz + nz, nz), xc, rows]
+        return remote(ref, ref, bsend.at[i], brecv.at[i], to)
+
+    rows_k, rows_b = pl.ds(0, BLK), pl.ds(0, held)
+    key_z = {d: k_copy(d, 0, d, rows_k, dev(z + d, x, c)) for d in direct}
+    bank_z = {d: b_copy(d, 0, rows_b, dev(z + d, x, c)) for d in direct}
+    relays = {}
+    if nz == 8:
+        up, down = (1, 2), (7, 6)
+        for i, source, target, part, parts_of, to in (
+            (3, 2, 3, 0, 1, up[0]), (5, 6, 5, 0, 1, down[0]),
+            (4, 2, 4, 0, 2, up[1]), (8, 6, 4, 1, 2, down[1]),
+        ):
+            rk = pl.ds(part * BLK // parts_of, BLK // parts_of)
+            rb_ = pl.ds(part * held // parts_of, held // parts_of)
+            key_z[i] = k_copy(i, source, target, rk, dev(z + to, x, c))
+            bank_z[i] = b_copy(i, -source if source < 4 else nz - source, rb_, dev(z + to, x, c))
+            relays.setdefault(source, []).append(i)
+
     key_core = {d: remote(kb.at[d, 0], kb.at[d, 1], dsend.at[d], drecv.at[d], sibling) for d in range(nz)}
     lo, hi = pl.ds(0, HEAD_CUT), pl.ds(HEAD_CUT, group - HEAD_CUT)
 
@@ -79,7 +125,6 @@
         q_copy(2, 0, 3, hi, west), q_copy(3, 0, 3, lo, west),
         q_copy(4, 1, 2, lo, east), q_copy(5, 3, 2, hi, west),
     ]
-    bank_z = {d: remote(bb.at[z, xc], bb.at[z, xc], bsend.at[d], brecv.at[d], dev(z + d, x, c)) for d in range(1, nz)}
     first, last = pl.ds(0, half_z), pl.ds(half_z, half_z)
 
     def c_copy(i, column, rows, target):
@@ -104,38 +149,46 @@
         return remote(bb.at[:, column(dx)], bb.at[:, column(dx)], es.at[dx], er.at[dx], sibling)
 
     bank_core = [e_copy(dx) for dx in range(NX)]
-
     near = [0, 1, nz - 1, 2][:per]
 
     def start_all():
         own[0].wait()
+        for d in direct:
+            key_z[d].start()
         key_core[0].start()
-        for d in sorted(range(1, nz), key=lambda d: (min(d, nz - d), d)):
-            key_z[d].start()
         own[1].wait()
-        for i in (0, 2, 1, 3):
-            q_x[i].start()
-        lhs_out[:, :hd] = qb[0].reshape(group * tok, hd)
-
-    def forward_key(*offsets):
-        for d in offsets:
-            if d in key_z:
-                key_z[d].wait_recv()
-                key_core[d].start()
+        q_x[0].start()
+        q_x[3].start()
+        own[4].wait()
+        prepare()
+
+    def second_part():
+        q_x[0].wait_send()
+        q_x[1].start()
+        q_x[3].wait_send()
+        q_x[2].start()
+
+    def pass_key(d):
+        key_z[d].wait_recv()
+        if d == 4 and nz == 8:
+            key_z[8].wait_recv()
+        for i in relays.get(d, ()):
+            key_z[i].start()
+        key_core[d].start()
+
+    def pass_bank(d):
+        bank_z[d].wait_recv()
+        for i in relays.get(d, ()):
+            bank_z[i].start()
 
     def have_keys(offsets):
         for d in offsets:
             key_core[d].wait_recv()
 
-    def forward_queries():
-        q_x[0].wait_recv()
-        q_x[4].start()
-        q_x[2].wait_recv()
-        q_x[5].start()
-
     def bank_rows():
-        for d in range(1, nz):
-            bank_z[d].wait_recv()
+        for i in bank_z:
+            if i not in relays:
+                bank_z[i].wait_recv()
         for i in (0, 2, 1, 3):
             bank_x[i].start()
         bank_core[0].start()
@@ -152,34 +205,41 @@
         bank_in[3].wait_recv()
         bank_core[1].start()
 
-    def at_step(step):
-        pair, g = step // groups, step % groups
-        if step == 0:
+    def before(pair, g, part):
+        if (pair, g, part) == (0, 0, 0):
             start_all()
-            forward_key(1)
-            if nz > 2:
-                forward_key(nz - 1, 2)
-            forward_queries()
+            second_part()
+            for d in direct[:2]:
+                pass_key(d)
             own[2].wait()
-            for d in range(1, nz):
+            for d in direct:
                 bank_z[d].start()
-            if nz > 4:
-                forward_key(nz - 2)
+            for d in direct[2:]:
+                pass_key(d)
+            q_x[0].wait_recv()
+            q_x[4].start()
             have_keys(near)
+            q_x[3].wait_recv()
+        if (pair, g, part) == (0, 0, 1):
+            q_x[2].wait_recv()
+            q_x[5].start()
+            for d in (3, 5) if nz == 8 else ():
+                pass_key(d)
+            for d in relays:
+                pass_bank(d)
             q_x[1].wait_recv()
-            q_x[3].wait_recv()
-        if pair == 0 and g == 1:
-            forward_key(3, nz - 3, 4)
+        if (pair, g, part) == (0, 1, 0):
+            pass_key(4)
             have_keys([d for d in range(nz) if d not in near])
-        if pair == 1 and g == 0:
+        if (pair, g, part) == (1, 0, 0):
+            q_x[4].wait_recv()
+        if (pair, g, part) == (1, 0, 1):
+            q_x[5].wait_recv()
             bank_rows()
-            q_x[4].wait_recv()
-            q_x[5].wait_recv()
 
     lane = lax.broadcasted_iota(jnp.int32, (1, BLK), 1)
 
-    def compute(step):
-        pair, g = step // groups, step % groups
+    def compute(pair, g, part):
         tiles = (1 - pair, 3 - pair)
         offsets = near if groups == 1 else [6 * g, 1 + 2 * g, 7 - 2 * g, 2 + 2 * g]
         members = [(d, rel) for d in offsets for rel in range(2)]
@@ -192,25 +252,33 @@
             first_in.append(hit[0])
             any_in.append((hit[0] | hit[1]).astype(jnp.float32))
         sums = [acc[d, rel] for d, rel in members]
-        for h in range(group):
+        for h in range(group)[HEAD_CUT:] if part else range(HEAD_CUT):
             rows = jnp.concatenate([qb[t, h] for t in tiles], axis=0)
             scores = lax.dot_general(
                 keys, rows, (((1,), (1,)), ((), ())), preferred_element_type=jnp.float32
             )
             for i in range(len(members)):
                 both = scores[i * BLK : (i + 1) * BLK]
-                part = jnp.where(first_in[i], both[:, :tok], both[:, tok:])
-                top = jnp.max(part, axis=0, keepdims=True)
-                e = jnp.exp2((part - top) * exp_scale)
+                part_scores = jnp.where(first_in[i], both[:, :tok], both[:, tok:])
+                top = jnp.max(part_scores, axis=0, keepdims=True)
+                e = jnp.exp2((part_scores - top) * exp_scale)
                 sums[i] = sums[i] + e * (any_in[i] / jnp.sum(e, axis=0, keepdims=True))
         for (d, rel), value in zip(members, sums):
             acc[d, rel] = value
 
-    @pl.loop(0, 2 * groups)
+    units = [(0, g, part) for g in range(groups) for part in range(2)]
+    units += [(1, g, part) for part in range(2) for g in range(groups)]
+
+    @pl.loop(0, len(units))
     def _(step):
-        for k in range(2 * groups):
-            pl.when(step == k)(functools.partial(at_step, k))
-        compute(step)
+        for k, unit in enumerate(units):
+            pl.when(step == k)(functools.partial(before, *unit))
+        pair = step // (2 * groups)
+        rest = lax.rem(step, 2 * groups)
+        g = jnp.where(pair == 0, rest // 2, lax.rem(rest, groups))
+        part = jnp.where(pair == 0, lax.rem(rest, 2), rest // groups)
+        for p in range(2):
+            pl.when(part == p)(functools.partial(compute, pair, g, p))
 
     for d in range(nz):
         for rel in range(2):
@@ -246,40 +314,33 @@
     bank_in[4].wait_recv()
     bank_in[5].wait_recv()
     bank_core[2].start()
+    for copy in [*key_z.values(), *key_core.values(), q_x[1], q_x[2], q_x[4], q_x[5], *bank_z.values(), *bank_x, *parts]:
+        copy.wait_send()
     for copy in bank_core:
-        copy.wait_recv()
-    columns = jnp.concatenate([slots[...], slots[...]], axis=1)
-    width = 2 * NX * b_hbm.shape[0]
-
-    def hits(first_row, count):
-        row = first_row + lax.broadcasted_iota(jnp.int32, (count, columns.shape[1]), 0)
-        chosen = (row == columns).astype(jnp.float32)
-        return chosen, jnp.max(chosen, axis=1, keepdims=True) > 0.5
+        copy.wait()
 
     @pl.loop(0, nz)
     def _(zz):
-        start = pl.multiple_of(zz * width, width)
-        chosen, taken = hits(start, width)
-        rest = jnp.where(taken, 0.0, bb[zz].reshape(width, hd).astype(jnp.float32))
-        rhs_out[pl.ds(start, width), :] = jnp.concatenate([rest, chosen], axis=1).astype(jnp.bfloat16)
-
+        start = pl.ds(pl.multiple_of(zz * width, width), width)
+        rhs_out[start, :hd] = bb[zz].reshape(width, hd) * keep[start, :]
+
+    chosen, taken = hits(s * held, held)
     for copy in sums_x:
         copy.wait_recv()
     ordered = [rx[pl.ds(zz, 2 * NX, stride=nz), :] for zz in range(nz)]
     reps = jnp.concatenate(ordered, axis=0).astype(jnp.bfloat16)
     value = lax.dot_general(
-        lhs_out[:, :hd], reps, (((1,), (1,)), ((), ())), preferred_element_type=jnp.float32
+        lhs_out[:, :hd], jnp.concatenate([reps, reps], axis=0), (((1,), (1,)), ((), ())),
+        preferred_element_type=jnp.float32,
     )
-    high = value.astype(jnp.bfloat16)
-    low = (value - high.astype(jnp.float32)).astype(jnp.bfloat16)
-    lhs_out[:, hd:] = jnp.concatenate([high, low], axis=1)
-    held = b_hbm.shape[0]
-    chosen, taken = hits(s * held, held)
+    high = value.astype(jnp.bfloat16).astype(jnp.float32)
+    left = lax.broadcasted_iota(jnp.int32, (1, 2 * reps.shape[0]), 1) < reps.shape[0]
+    lhs_out[:, hd:] = jnp.where(left, high, value - high).astype(jnp.bfloat16)
     placed = jnp.dot(
         chosen[:, : reps.shape[0]].astype(jnp.bfloat16), reps, preferred_element_type=jnp.float32
     )
-    shard_out[...] = jnp.where(taken, placed, bb[z, xc].astype(jnp.float32)).astype(jnp.bfloat16)
-    for copy in [*key_z.values(), *key_core.values(), *q_x, *bank_z.values(), *bank_x, *bank_core, *parts, *sums_x]:
+    shard_out[...] = jnp.where(taken > 0.5, placed, bb[z, xc].astype(jnp.float32)).astype(jnp.bfloat16)
+    for copy in sums_x:
         copy.wait_send()
 
 
@@ -296,20 +357,23 @@
             on_chip((group * tok, hd + 2 * slots.shape[1]), jnp.bfloat16),
             on_chip(b.shape, jnp.bfloat16),
         ),
-        in_specs=[pl.BlockSpec(memory_space=pltpu.SMEM), vmem, hbm, hbm, hbm],
+        in_specs=[hbm] * 5,
         out_specs=(vmem, vmem, vmem),
         scratch_shapes=[
+            pltpu.SMEM(window_start.shape, jnp.int32),
+            VMEM(slots.shape, jnp.int32),
             VMEM((NX, group, tok, hd), jnp.bfloat16),
             VMEM((nz, 2, BLK, hd), jnp.bfloat16),
             VMEM(bank_shape, jnp.bfloat16),
+            VMEM((nz * 2 * NX * b.shape[0], hd), jnp.bfloat16),
             VMEM((nz, 2, BLK, BLK), jnp.float32),
             VMEM((2, nz, hd), jnp.float32),
             VMEM((2 * nz, nz, hd), jnp.float32),
             VMEM((2 * NX * nz, hd), jnp.float32),
-            dma((3,)),
-            dma((nz,)), dma((nz,)), dma((nz,)), dma((nz,)),
+            dma((5,)),
+            dma((nz + 1,)), dma((nz + 1,)), dma((nz,)), dma((nz,)),
             dma((6,)), dma((6,)),
-            dma((nz,)), dma((nz,)),
+            dma((nz + 1,)), dma((nz + 1,)),
             dma((6,)), dma((6,)), dma((NX,)), dma((NX,)),
             dma((2 * nz,)), dma((2 * nz,)), dma((2 * NX,)), dma((2 * NX,)),
         ],

time: 41.6 us -> 38.2 us (0.918)
  Pallas kernels: 40.9 us -> 37.5 us
    pallas_call x1, Pallas kernels: 37.4 us -> 34 us  [refresh(): pl.pallas_call(functools.partial(refresh_kernel, nz), out_shape=(on_chip(...]
where the time goes in v3:
time: 38.2 us; the launch traced here: 38.1 us
  Pallas kernels  37.5 us (98%)
  between operations  0.64 us (2%)
    pallas_call x1, Pallas kernels, refresh(): pl.pallas_call(functools.partial(refresh_kernel, nz), out_shape=(on_chip(...  34 us
    pallas_call x1, Pallas kernels, relevance_of(): pl.pallas_call(functools.partial(relevance_kernel, tile), out_shape=(jax....  3.5 us

profile of v3, /device:TPU:1, one launch (start us, length us, event | category | flops | bytes accessed | tf_op | source)
XLA Modules:
  0.0 38.1 jit_solution(14740448548794430728)
XLA Ops:
  0.6 34.0 %refresh.1 = (bf16[4096,256]{1,0:T(8,128)(2,1)S(1)}, bf16[896,256]{1,0:T(8,128)(2,1)S(1)}, bf16[64,128]{1,0:T(8,128)(2,1)S(1)}) custom-call(s32[64]{0:T(128)} %ws_hbm.1, s32[1,64]{1,0:T(1,128)} %bitcast.11, bf16[7,128,128]{2,1,0:T(8,128)(2,1)} %bitcast.8, bf16[128,128]{1,0:T(8,128)(2,1)} %bitcast.9, bf16[64,128]{1,0:T(8,128)(2,1)} %bitcast.10), custom_call_target="tpu_custom_call" | custom-call | tf_op jit(solution)/shard_map/refresh/pallas_call | solution.py:353
  34.6 3.5 %relevance.1 = (bf16[896,4096]{1,0:T(8,128)(2,1)}, bf16[64,128]{1,0:T(8,128)(2,1)}) custom-call(bf16[896,256]{1,0:T(8,128)(2,1)S(1)} %get-tuple-element.7.lhs, bf16[4096,256]{1,0:T(8,128)(2,1)S(1)} %get-tuple-element.8.rhs, bf16[64,128]{1,0:T(8,128)(2,1)S(1)} %get-tuple-element.9.shard), custom_call_target="tpu_custom_call" | custom-call | tf_op jit(solution)/shard_map/relevance/pallas_call | solution.py:407

commit v4 on v3

--- a/solution.py
+++ b/solution.py
@@ -27,8 +27,7 @@
 def refresh_kernel(
     nz, ws_hbm, slots_hbm, q_hbm, k_hbm, b_hbm, rhs_out, lhs_out, shard_out,
     ws, slots, qb, kb, bb, keep, acc, pb, rb, rx,
-    lsem, ksend, krecv, dsend, drecv, qsend, qrecv, bsend, brecv,
-    cs, cr, es, er, ps, pr, xs, xr,
+    lsem, sent, come, krecv, drecv, qsend, qrecv, brecv, cr,
 ):
     group, tok, hd = q_hbm.shape
     held = b_hbm.shape[0]
@@ -92,11 +91,11 @@
         lhs_out[:, :hd] = qb[0].reshape(group * tok, hd)
 
     def k_copy(i, source, target, rows, to):
-        return remote(kb.at[source, 0, rows], kb.at[target, 0, rows], ksend.at[i], krecv.at[i], to)
+        return remote(kb.at[source, 0, rows], kb.at[target, 0, rows], sent.at[0], krecv.at[i], to)
 
     def b_copy(i, dz, rows, to):
         ref = bb.at[lax.rem(z + dz + nz, nz), xc, rows]
-        return remote(ref, ref, bsend.at[i], brecv.at[i], to)
+        return remote(ref, ref, sent.at[1], brecv.at[i], to)
 
     rows_k, rows_b = pl.ds(0, BLK), pl.ds(0, held)
     key_z = {d: k_copy(d, 0, d, rows_k, dev(z + d, x, c)) for d in direct}
@@ -114,7 +113,7 @@
             bank_z[i] = b_copy(i, -source if source < 4 else nz - source, rb_, dev(z + to, x, c))
             relays.setdefault(source, []).append(i)
 
-    key_core = {d: remote(kb.at[d, 0], kb.at[d, 1], dsend.at[d], drecv.at[d], sibling) for d in range(nz)}
+    key_core = {d: remote(kb.at[d, 0], kb.at[d, 1], sent.at[2], drecv.at[d], sibling) for d in range(nz)}
     lo, hi = pl.ds(0, HEAD_CUT), pl.ds(HEAD_CUT, group - HEAD_CUT)
 
     def q_copy(i, src_slot, dst_slot, heads, target):
@@ -128,7 +127,7 @@
     first, last = pl.ds(0, half_z), pl.ds(half_z, half_z)
 
     def c_copy(i, column, rows, target):
-        return remote(bb.at[rows, column], bb.at[rows, column], cs.at[i], cr.at[i], target)
+        return remote(bb.at[rows, column], bb.at[rows, column], sent.at[3], cr.at[i], target)
 
     def column(dx):
         return lax.rem(x + dx, NX) * 2 + c
@@ -146,7 +145,7 @@
     ]
 
     def e_copy(dx):
-        return remote(bb.at[:, column(dx)], bb.at[:, column(dx)], es.at[dx], er.at[dx], sibling)
+        return remote(bb.at[:, column(dx)], bb.at[:, column(dx)], sent.at[4], come.at[0], sibling)
 
     bank_core = [e_copy(dx) for dx in range(NX)]
     near = [0, 1, nz - 1, 2][:per]
@@ -205,7 +204,7 @@
         bank_in[3].wait_recv()
         bank_core[1].start()
 
-    def before(pair, g, part):
+    def before(pair, g, part=0):
         if (pair, g, part) == (0, 0, 0):
             start_all()
             second_part()
@@ -228,18 +227,17 @@
             for d in relays:
                 pass_bank(d)
             q_x[1].wait_recv()
-        if (pair, g, part) == (0, 1, 0):
+        if (pair, g) == (0, 1):
             pass_key(4)
             have_keys([d for d in range(nz) if d not in near])
-        if (pair, g, part) == (1, 0, 0):
+        if (pair, g) == (1, 0):
             q_x[4].wait_recv()
-        if (pair, g, part) == (1, 0, 1):
             q_x[5].wait_recv()
             bank_rows()
 
     lane = lax.broadcasted_iota(jnp.int32, (1, BLK), 1)
 
-    def compute(pair, g, part):
+    def compute(pair, g, heads):
         tiles = (1 - pair, 3 - pair)
         offsets = near if groups == 1 else [6 * g, 1 + 2 * g, 7 - 2 * g, 2 + 2 * g]
         members = [(d, rel) for d in offsets for rel in range(2)]
@@ -252,7 +250,7 @@
             first_in.append(hit[0])
             any_in.append((hit[0] | hit[1]).astype(jnp.float32))
         sums = [acc[d, rel] for d, rel in members]
-        for h in range(group)[HEAD_CUT:] if part else range(HEAD_CUT):
+        for h in heads:
             rows = jnp.concatenate([qb[t, h] for t in tiles], axis=0)
             scores = lax.dot_general(
                 keys, rows, (((1,), (1,)), ((), ())), preferred_element_type=jnp.float32
@@ -266,19 +264,16 @@
         for (d, rel), value in zip(members, sums):
             acc[d, rel] = value
 
-    units = [(0, g, part) for g in range(groups) for part in range(2)]
-    units += [(1, g, part) for part in range(2) for g in range(groups)]
-
-    @pl.loop(0, len(units))
+    before(0, 0, 0)
+    compute(0, 0, range(HEAD_CUT))
+    before(0, 0, 1)
+    compute(0, 0, range(HEAD_CUT, group))
+
+    @pl.loop(1, 2 * groups)
     def _(step):
-        for k, unit in enumerate(units):
-            pl.when(step == k)(functools.partial(before, *unit))
-        pair = step // (2 * groups)
-        rest = lax.rem(step, 2 * groups)
-        g = jnp.where(pair == 0, rest // 2, lax.rem(rest, groups))
-        part = jnp.where(pair == 0, lax.rem(rest, 2), rest // groups)
-        for p in range(2):
-            pl.when(part == p)(functools.partial(compute, pair, g, p))
+        for k in range(1, 2 * groups):
+            pl.when(step == k)(functools.partial(before, k // groups, k % groups))
+        compute(step // groups, lax.rem(step, groups), range(group))
 
     for d in range(nz):
         for rel in range(2):
@@ -288,7 +283,7 @@
 
     column_peers = [(dz, dc) for dz in range(nz) for dc in range(2) if dz or dc]
     parts = [
-        remote(pb.at[(c + dc) % 2], rb.at[dz * 2 + dc], ps.at[dz * 2 + dc], pr.at[dz * 2 + dc], dev(z + dz, x, (c + dc) % 2))
+        remote(pb.at[(c + dc) % 2], rb.at[dz * 2 + dc], sent.at[5], come.at[1], dev(z + dz, x, (c + dc) % 2))
         for dz, dc in column_peers
     ]
     for copy in parts:
@@ -296,8 +291,17 @@
     rb[0] = pb[c]
     bank_forward()
     bank_cross()
-    for copy in parts:
-        copy.wait_recv()
+    def together(ref, i, j=0):
+        return remote(ref, ref, sent.at[i], come.at[j], sibling)
+
+    all_keys = together(kb.at[pl.ds(0, nz - 1), 0], 0)
+    all_shards = together(bb.at[pl.ds(0, nz - 1), 0], 1)
+    all_key_core = together(kb.at[:, 0], 2)
+    all_bank_x = together(bb.at[:, pl.ds(0, 3)], 3)
+    all_bank_core = together(bb.at[:, pl.ds(0, NX)], 4, 0)
+    all_parts = together(rb.at[pl.ds(1, 2 * nz - 1)], 5, 1)
+    all_sums = together(rx.at[pl.ds(0, (2 * NX - 1) * nz)], 6, 2)
+    all_parts.wait_recv()
     total = jnp.zeros((nz, hd), jnp.float32)
     for dz in range(nz):
         for dc in range(2):
@@ -306,7 +310,7 @@
     rx[mine, :] = total / (group * WIN)
     row_peers = [(dx, dc) for dx in range(NX) for dc in range(2) if dx or dc]
     sums_x = [
-        remote(rx.at[mine], rx.at[mine], xs.at[dx * 2 + dc], xr.at[dx * 2 + dc], dev(z, x + dx, (c + dc) % 2))
+        remote(rx.at[mine], rx.at[mine], sent.at[6], come.at[2], dev(z, x + dx, (c + dc) % 2))
         for dx, dc in row_peers
     ]
     for copy in sums_x:
@@ -314,10 +318,9 @@
     bank_in[4].wait_recv()
     bank_in[5].wait_recv()
     bank_core[2].start()
-    for copy in [*key_z.values(), *key_core.values(), q_x[1], q_x[2], q_x[4], q_x[5], *bank_z.values(), *bank_x, *parts]:
+    for copy in (all_keys, all_shards, all_key_core, all_bank_x, all_parts, q_x[1], q_x[2], q_x[4], q_x[5]):
         copy.wait_send()
-    for copy in bank_core:
-        copy.wait()
+    all_bank_core.wait()
 
     @pl.loop(0, nz)
     def _(zz):
@@ -325,8 +328,7 @@
         rhs_out[start, :hd] = bb[zz].reshape(width, hd) * keep[start, :]
 
     chosen, taken = hits(s * held, held)
-    for copy in sums_x:
-        copy.wait_recv()
+    all_sums.wait_recv()
     ordered = [rx[pl.ds(zz, 2 * NX, stride=nz), :] for zz in range(nz)]
     reps = jnp.concatenate(ordered, axis=0).astype(jnp.bfloat16)
     value = lax.dot_general(
@@ -340,8 +342,7 @@
         chosen[:, : reps.shape[0]].astype(jnp.bfloat16), reps, preferred_element_type=jnp.float32
     )
     shard_out[...] = jnp.where(taken > 0.5, placed, bb[z, xc].astype(jnp.float32)).astype(jnp.bfloat16)
-    for copy in sums_x:
-        copy.wait_send()
+    all_sums.wait_send()
 
 
 def refresh(nz, window_start, slots, q, k, b):
@@ -370,12 +371,8 @@
             VMEM((2, nz, hd), jnp.float32),
             VMEM((2 * nz, nz, hd), jnp.float32),
             VMEM((2 * NX * nz, hd), jnp.float32),
-            dma((5,)),
-            dma((nz + 1,)), dma((nz + 1,)), dma((nz,)), dma((nz,)),
-            dma((6,)), dma((6,)),
-            dma((nz + 1,)), dma((nz + 1,)),
-            dma((6,)), dma((6,)), dma((NX,)), dma((NX,)),
-            dma((2 * nz,)), dma((2 * nz,)), dma((2 * NX,)), dma((2 * NX,)),
+            dma((5,)), dma((7,)), dma((3,)),
+            dma((nz + 1,)), dma((nz,)), dma((6,)), dma((6,)), dma((nz + 1,)), dma((6,)),
         ],
         compiler_params=pltpu.CompilerParams(collective_id=0, has_side_effects=True),
         name="refresh",

time: 38.2 us -> 37.2 us (0.974)
  Pallas kernels: 37.5 us -> 36.5 us
    pallas_call x1, Pallas kernels: 34 us -> 33 us  [refresh(): pl.pallas_call(functools.partial(refresh_kernel, nz), out_shape=(on_chip(...]
where the time goes in v4:
time: 37.2 us
  Pallas kernels  36.5 us (98%)
  between operations  0.64 us (2%)
    pallas_call x1, Pallas kernels, refresh(): pl.pallas_call(functools.partial(refresh_kernel, nz), out_shape=(on_chip(...  33 us
    pallas_call x1, Pallas kernels, relevance_of(): pl.pallas_call(functools.partial(relevance_kernel, tile), out_shape=(jax....  3.5 us

profile of v4, /device:TPU:1, one launch (start us, length us, event | category | flops | bytes accessed | tf_op | source)
XLA Modules:
  0.0 37.2 jit_solution(9637120094026608138)
XLA Ops:
  0.6 33.0 %refresh.1 = (bf16[4096,256]{1,0:T(8,128)(2,1)S(1)}, bf16[896,256]{1,0:T(8,128)(2,1)S(1)}, bf16[64,128]{1,0:T(8,128)(2,1)S(1)}) custom-call(s32[64]{0:T(128)} %ws_hbm.1, s32[1,64]{1,0:T(1,128)} %bitcast.11, bf16[7,128,128]{2,1,0:T(8,128)(2,1)} %bitcast.8, bf16[128,128]{1,0:T(8,128)(2,1)} %bitcast.9, bf16[64,128]{1,0:T(8,128)(2,1)} %bitcast.10), custom_call_target="tpu_custom_call" | custom-call | tf_op jit(solution)/shard_map/refresh/pallas_call | solution.py:354
  33.7 3.5 %relevance.1 = (bf16[896,4096]{1,0:T(8,128)(2,1)}, bf16[64,128]{1,0:T(8,128)(2,1)}) custom-call(bf16[896,256]{1,0:T(8,128)(2,1)S(1)} %get-tuple-element.7.lhs, bf16[4096,256]{1,0:T(8,128)(2,1)S(1)} %get-tuple-element.8.rhs, bf16[64,128]{1,0:T(8,128)(2,1)S(1)} %get-tuple-element.9.shard), custom_call_target="tpu_custom_call" | custom-call | tf_op jit(solution)/shard_map/relevance/pallas_call | solution.py:404

commit v5 on v4

--- a/solution.py
+++ b/solution.py
@@ -27,7 +27,7 @@
 def refresh_kernel(
     nz, ws_hbm, slots_hbm, q_hbm, k_hbm, b_hbm, rhs_out, lhs_out, shard_out,
     ws, slots, qb, kb, bb, keep, acc, pb, rb, rx,
-    lsem, sent, come, krecv, drecv, qsend, qrecv, brecv, cr,
+    lsem, sent, come, krecv, qsend, qrecv, brecv, cr,
 ):
     group, tok, hd = q_hbm.shape
     held = b_hbm.shape[0]
@@ -95,7 +95,7 @@
 
     def b_copy(i, dz, rows, to):
         ref = bb.at[lax.rem(z + dz + nz, nz), xc, rows]
-        return remote(ref, ref, sent.at[1], brecv.at[i], to)
+        return remote(ref, ref, sent.at[1], come.at[5] if i not in (2, 6) else brecv.at[i // 6], to)
 
     rows_k, rows_b = pl.ds(0, BLK), pl.ds(0, held)
     key_z = {d: k_copy(d, 0, d, rows_k, dev(z + d, x, c)) for d in direct}
@@ -113,7 +113,8 @@
             bank_z[i] = b_copy(i, -source if source < 4 else nz - source, rb_, dev(z + to, x, c))
             relays.setdefault(source, []).append(i)
 
-    key_core = {d: remote(kb.at[d, 0], kb.at[d, 1], sent.at[2], drecv.at[d], sibling) for d in range(nz)}
+    near = [0, 1, nz - 1, 2][:per]
+    key_core = {d: remote(kb.at[d, 0], kb.at[d, 1], sent.at[2], come.at[3 if d in near else 4], sibling) for d in range(nz)}
     lo, hi = pl.ds(0, HEAD_CUT), pl.ds(HEAD_CUT, group - HEAD_CUT)
 
     def q_copy(i, src_slot, dst_slot, heads, target):
@@ -148,7 +149,20 @@
         return remote(bb.at[:, column(dx)], bb.at[:, column(dx)], sent.at[4], come.at[0], sibling)
 
     bank_core = [e_copy(dx) for dx in range(NX)]
-    near = [0, 1, nz - 1, 2][:per]
+
+    def together(ref, i, j=0):
+        return remote(ref, ref, sent.at[i], come.at[j], sibling)
+
+    all_keys = together(kb.at[pl.ds(0, nz - 1), 0], 0)
+    all_shards = together(bb.at[pl.ds(0, nz - 1), 0], 1)
+    all_key_core = together(kb.at[:, 0], 2)
+    all_bank_x = together(bb.at[:, pl.ds(0, 3)], 3)
+    all_bank_core = together(bb.at[:, pl.ds(0, NX)], 4, 0)
+    all_parts = together(rb.at[pl.ds(1, 2 * nz - 1)], 5, 1)
+    all_sums = together(rx.at[pl.ds(0, (2 * NX - 1) * nz)], 6, 2)
+    near_keys = together(kb.at[pl.ds(0, per), 1], 2, 3)
+    far_keys = together(kb.at[pl.ds(0, nz - per), 1], 2, 4) if groups > 1 else None
+    rest_shards = together(bb.at[pl.ds(0, nz - 1 - len([d for d in direct if d in (2, 6)])), 0], 1, 5)
 
     def start_all():
         own[0].wait()
@@ -180,13 +194,10 @@
         for i in relays.get(d, ()):
             bank_z[i].start()
 
-    def have_keys(offsets):
-        for d in offsets:
-            key_core[d].wait_recv()
-
     def bank_rows():
-        for i in bank_z:
-            if i not in relays:
+        rest_shards.wait_recv()
+        for i in (2, 6):
+            if i in bank_z and i not in relays:
                 bank_z[i].wait_recv()
         for i in (0, 2, 1, 3):
             bank_x[i].start()
@@ -210,29 +221,33 @@
             second_part()
             for d in direct[:2]:
                 pass_key(d)
-            own[2].wait()
-            for d in direct:
-                bank_z[d].start()
             for d in direct[2:]:
                 pass_key(d)
             q_x[0].wait_recv()
             q_x[4].start()
-            have_keys(near)
+            near_keys.wait_recv()
+            own[2].wait()
+            for d in direct:
+                bank_z[d].start()
             q_x[3].wait_recv()
         if (pair, g, part) == (0, 0, 1):
             q_x[2].wait_recv()
             q_x[5].start()
             for d in (3, 5) if nz == 8 else ():
                 pass_key(d)
+            q_x[1].wait_recv()
+            if nz == 8:
+                pass_key(4)
+        if (pair, g) == (0, 1):
+            far_keys.wait_recv()
             for d in relays:
                 pass_bank(d)
-            q_x[1].wait_recv()
-        if (pair, g) == (0, 1):
-            pass_key(4)
-            have_keys([d for d in range(nz) if d not in near])
         if (pair, g) == (1, 0):
             q_x[4].wait_recv()
             q_x[5].wait_recv()
+            if groups == 1:
+                bank_rows()
+        if groups > 1 and (pair, g) == (1, groups - 1):
             bank_rows()
 
     lane = lax.broadcasted_iota(jnp.int32, (1, BLK), 1)
@@ -269,19 +284,29 @@
     before(0, 0, 1)
     compute(0, 0, range(HEAD_CUT, group))
 
-    @pl.loop(1, 2 * groups)
+    final = 2 * groups - 1
+
+    @pl.loop(1, final)
     def _(step):
-        for k in range(1, 2 * groups):
+        for k in range(1, final):
             pl.when(step == k)(functools.partial(before, k // groups, k % groups))
         compute(step // groups, lax.rem(step, groups), range(group))
 
-    for d in range(nz):
-        for rel in range(2):
-            weight = jnp.sum(acc[d, rel], axis=1, keepdims=True)
-            row = jnp.sum(weight * kb[d, rel].astype(jnp.float32), axis=0, keepdims=True)
-            pb[(c + rel) % 2, pl.ds(lax.rem(z - d + nz, nz), 1), :] = row
+    def partial(offsets):
+        for d in offsets:
+            for rel in range(2):
+                weight = jnp.sum(acc[d, rel], axis=1, keepdims=True)
+                row = jnp.sum(weight * kb[d, rel].astype(jnp.float32), axis=0, keepdims=True)
+                pb[(c + rel) % 2, pl.ds(lax.rem(z - d + nz, nz), 1), :] = row
+
+    before(1, groups - 1)
+    compute(1, groups - 1, range(group))
+    if groups > 1:
+        partial(near)
+    partial([d for d in range(nz) if groups == 1 or d not in near])
 
     column_peers = [(dz, dc) for dz in range(nz) for dc in range(2) if dz or dc]
+    column_peers.sort(key=lambda p: -min(p[0], nz - p[0]))
     parts = [
         remote(pb.at[(c + dc) % 2], rb.at[dz * 2 + dc], sent.at[5], come.at[1], dev(z + dz, x, (c + dc) % 2))
         for dz, dc in column_peers
@@ -291,16 +316,6 @@
     rb[0] = pb[c]
     bank_forward()
     bank_cross()
-    def together(ref, i, j=0):
-        return remote(ref, ref, sent.at[i], come.at[j], sibling)
-
-    all_keys = together(kb.at[pl.ds(0, nz - 1), 0], 0)
-    all_shards = together(bb.at[pl.ds(0, nz - 1), 0], 1)
-    all_key_core = together(kb.at[:, 0], 2)
-    all_bank_x = together(bb.at[:, pl.ds(0, 3)], 3)
-    all_bank_core = together(bb.at[:, pl.ds(0, NX)], 4, 0)
-    all_parts = together(rb.at[pl.ds(1, 2 * nz - 1)], 5, 1)
-    all_sums = together(rx.at[pl.ds(0, (2 * NX - 1) * nz)], 6, 2)
     all_parts.wait_recv()
     total = jnp.zeros((nz, hd), jnp.float32)
     for dz in range(nz):
@@ -309,6 +324,7 @@
     mine = pl.ds(pl.multiple_of(xc * nz, nz), nz)
     rx[mine, :] = total / (group * WIN)
     row_peers = [(dx, dc) for dx in range(NX) for dc in range(2) if dx or dc]
+    row_peers.sort(key=lambda p: -min(p[0], NX - p[0]))
     sums_x = [
         remote(rx.at[mine], rx.at[mine], sent.at[6], come.at[2], dev(z, x + dx, (c + dc) % 2))
         for dx, dc in row_peers
@@ -371,8 +387,8 @@
             VMEM((2, nz, hd), jnp.float32),
             VMEM((2 * nz, nz, hd), jnp.float32),
             VMEM((2 * NX * nz, hd), jnp.float32),
-            dma((5,)), dma((7,)), dma((3,)),
-            dma((nz + 1,)), dma((nz,)), dma((6,)), dma((6,)), dma((nz + 1,)), dma((6,)),
+            dma((5,)), dma((7,)), dma((6,)),
+            dma((nz + 1,)), dma((6,)), dma((6,)), dma((2,)), dma((6,)),
         ],
         compiler_params=pltpu.CompilerParams(collective_id=0, has_side_effects=True),
         name="refresh",

time: 37.2 us -> 36.5 us (0.981)
  Pallas kernels: 36.5 us -> 35.8 us
    pallas_call x1, Pallas kernels: 33 us -> 32.3 us  [refresh(): pl.pallas_call(functools.partial(refresh_kernel, nz), out_shape=(on_chip(...]
where the time goes in v5:
time: 36.5 us; the launch traced here: 36.4 us
  Pallas kernels  35.8 us (98%)
  between operations  0.64 us (2%)
    pallas_call x1, Pallas kernels, refresh(): pl.pallas_call(functools.partial(refresh_kernel, nz), out_shape=(on_chip(...  32.3 us
    pallas_call x1, Pallas kernels, relevance_of(): pl.pallas_call(functools.partial(relevance_kernel, tile), out_shape=(jax....  3.5 us

profile of v5, /device:TPU:1, one launch (start us, length us, event | category | flops | bytes accessed | tf_op | source)
XLA Modules:
  0.0 36.4 jit_solution(1176926008674735058)
XLA Ops:
  0.6 32.3 %refresh.1 = (bf16[4096,256]{1,0:T(8,128)(2,1)S(1)}, bf16[896,256]{1,0:T(8,128)(2,1)S(1)}, bf16[64,128]{1,0:T(8,128)(2,1)S(1)}) custom-call(s32[64]{0:T(128)} %ws_hbm.1, s32[1,64]{1,0:T(1,128)} %bitcast.11, bf16[7,128,128]{2,1,0:T(8,128)(2,1)} %bitcast.8, bf16[128,128]{1,0:T(8,128)(2,1)} %bitcast.9, bf16[64,128]{1,0:T(8,128)(2,1)} %bitcast.10), custom_call_target="tpu_custom_call" | custom-call | tf_op jit(solution)/shard_map/refresh/pallas_call | solution.py:370
  32.9 3.5 %relevance.1 = (bf16[896,4096]{1,0:T(8,128)(2,1)}, bf16[64,128]{1,0:T(8,128)(2,1)}) custom-call(bf16[896,256]{1,0:T(8,128)(2,1)S(1)} %get-tuple-element.7.lhs, bf16[4096,256]{1,0:T(8,128)(2,1)S(1)} %get-tuple-element.8.rhs, bf16[64,128]{1,0:T(8,128)(2,1)S(1)} %get-tuple-element.9.shard), custom_call_target="tpu_custom_call" | custom-call | tf_op jit(solution)/shard_map/relevance/pallas_call | solution.py:420

commit v6 on v5

--- a/solution.py
+++ b/solution.py
@@ -27,7 +27,7 @@
 def refresh_kernel(
     nz, ws_hbm, slots_hbm, q_hbm, k_hbm, b_hbm, rhs_out, lhs_out, shard_out,
     ws, slots, qb, kb, bb, keep, acc, pb, rb, rx,
-    lsem, sent, come, krecv, qsend, qrecv, brecv, cr,
+    lsem, sent, come, krecv, qsend, qrecv, cr,
 ):
     group, tok, hd = q_hbm.shape
     held = b_hbm.shape[0]
@@ -95,11 +95,11 @@
 
     def b_copy(i, dz, rows, to):
         ref = bb.at[lax.rem(z + dz + nz, nz), xc, rows]
-        return remote(ref, ref, sent.at[1], come.at[5] if i not in (2, 6) else brecv.at[i // 6], to)
+        return remote(ref, ref, sent.at[1], come.at[5], to)
 
     rows_k, rows_b = pl.ds(0, BLK), pl.ds(0, held)
     key_z = {d: k_copy(d, 0, d, rows_k, dev(z + d, x, c)) for d in direct}
-    bank_z = {d: b_copy(d, 0, rows_b, dev(z + d, x, c)) for d in direct}
+    bank_z = {d: b_copy(0, 0, rows_b, dev(z + d, x, c)) for d in range(1, nz)}
     relays = {}
     if nz == 8:
         up, down = (1, 2), (7, 6)
@@ -108,9 +108,7 @@
             (4, 2, 4, 0, 2, up[1]), (8, 6, 4, 1, 2, down[1]),
         ):
             rk = pl.ds(part * BLK // parts_of, BLK // parts_of)
-            rb_ = pl.ds(part * held // parts_of, held // parts_of)
             key_z[i] = k_copy(i, source, target, rk, dev(z + to, x, c))
-            bank_z[i] = b_copy(i, -source if source < 4 else nz - source, rb_, dev(z + to, x, c))
             relays.setdefault(source, []).append(i)
 
     near = [0, 1, nz - 1, 2][:per]
@@ -162,7 +160,7 @@
     all_sums = together(rx.at[pl.ds(0, (2 * NX - 1) * nz)], 6, 2)
     near_keys = together(kb.at[pl.ds(0, per), 1], 2, 3)
     far_keys = together(kb.at[pl.ds(0, nz - per), 1], 2, 4) if groups > 1 else None
-    rest_shards = together(bb.at[pl.ds(0, nz - 1 - len([d for d in direct if d in (2, 6)])), 0], 1, 5)
+    rest_shards = together(bb.at[pl.ds(0, nz - 1), 0], 1, 5)
 
     def start_all():
         own[0].wait()
@@ -189,16 +187,8 @@
             key_z[i].start()
         key_core[d].start()
 
-    def pass_bank(d):
-        bank_z[d].wait_recv()
-        for i in relays.get(d, ()):
-            bank_z[i].start()
-
     def bank_rows():
         rest_shards.wait_recv()
-        for i in (2, 6):
-            if i in bank_z and i not in relays:
-                bank_z[i].wait_recv()
         for i in (0, 2, 1, 3):
             bank_x[i].start()
         bank_core[0].start()
@@ -233,15 +223,14 @@
         if (pair, g, part) == (0, 0, 1):
             q_x[2].wait_recv()
             q_x[5].start()
-            for d in (3, 5) if nz == 8 else ():
+            for d in (3, 5, 4) if nz == 8 else ():
                 pass_key(d)
+            for d in range(1, nz):
+                if d not in direct:
+                    bank_z[d].start()
             q_x[1].wait_recv()
-            if nz == 8:
-                pass_key(4)
         if (pair, g) == (0, 1):
             far_keys.wait_recv()
-            for d in relays:
-                pass_bank(d)
         if (pair, g) == (1, 0):
             q_x[4].wait_recv()
             q_x[5].wait_recv()
@@ -388,7 +377,7 @@
             VMEM((2 * nz, nz, hd), jnp.float32),
             VMEM((2 * NX * nz, hd), jnp.float32),
             dma((5,)), dma((7,)), dma((6,)),
-            dma((nz + 1,)), dma((6,)), dma((6,)), dma((2,)), dma((6,)),
+            dma((nz + 1,)), dma((6,)), dma((6,)), dma((6,)),
         ],
         compiler_params=pltpu.CompilerParams(collective_id=0, has_side_effects=True),
         name="refresh",

time: 36.5 us -> 36.4 us (level)
  no operation moved by 1% of the time
where the time goes in v6:
time: 36.4 us; the launch traced here: 36.3 us
  Pallas kernels  35.7 us (98%)
  between operations  0.64 us (2%)
    pallas_call x1, Pallas kernels, refresh(): pl.pallas_call(functools.partial(refresh_kernel, nz), out_shape=(on_chip(...  32.2 us
    pallas_call x1, Pallas kernels, relevance_of(): pl.pallas_call(functools.partial(relevance_kernel, tile), out_shape=(jax....  3.5 us

profile of v6, /device:TPU:1, one launch (start us, length us, event | category | flops | bytes accessed | tf_op | source)
XLA Modules:
  0.0 36.3 jit_solution(7158468860693573566)
XLA Ops:
  0.6 32.2 %refresh.1 = (bf16[4096,256]{1,0:T(8,128)(2,1)S(1)}, bf16[896,256]{1,0:T(8,128)(2,1)S(1)}, bf16[64,128]{1,0:T(8,128)(2,1)S(1)}) custom-call(s32[64]{0:T(128)} %ws_hbm.1, s32[1,64]{1,0:T(1,128)} %bitcast.11, bf16[7,128,128]{2,1,0:T(8,128)(2,1)} %bitcast.8, bf16[128,128]{1,0:T(8,128)(2,1)} %bitcast.9, bf16[64,128]{1,0:T(8,128)(2,1)} %bitcast.10), custom_call_target="tpu_custom_call" | custom-call | tf_op jit(solution)/shard_map/refresh/pallas_call | solution.py:359
  32.8 3.5 %relevance.1 = (bf16[896,4096]{1,0:T(8,128)(2,1)}, bf16[64,128]{1,0:T(8,128)(2,1)}) custom-call(bf16[896,256]{1,0:T(8,128)(2,1)S(1)} %get-tuple-element.7.lhs, bf16[4096,256]{1,0:T(8,128)(2,1)S(1)} %get-tuple-element.8.rhs, bf16[64,128]{1,0:T(8,128)(2,1)S(1)} %get-tuple-element.9.shard), custom_call_target="tpu_custom_call" | custom-call | tf_op jit(solution)/shard_map/relevance/pallas_call | solution.py:409

commit v7 on v6

--- a/solution.py
+++ b/solution.py
@@ -273,13 +273,9 @@
     before(0, 0, 1)
     compute(0, 0, range(HEAD_CUT, group))
 
-    final = 2 * groups - 1
-
-    @pl.loop(1, final)
-    def _(step):
-        for k in range(1, final):
-            pl.when(step == k)(functools.partial(before, k // groups, k % groups))
-        compute(step // groups, lax.rem(step, groups), range(group))
+    for k in range(1, 2 * groups - 1):
+        before(k // groups, k % groups)
+        compute(k // groups, k % groups, range(group))
 
     def partial(offsets):
         for d in offsets:

time: 36.4 us -> 36.4 us (level)
  no operation moved by 1% of the time
where the time goes in v7:
time: 36.4 us; the launch traced here: 36.3 us
  Pallas kernels  35.7 us (98%)
  between operations  0.64 us (2%)
    pallas_call x1, Pallas kernels, refresh(): pl.pallas_call(functools.partial(refresh_kernel, nz), out_shape=(on_chip(...  32.2 us
    pallas_call x1, Pallas kernels, relevance_of(): pl.pallas_call(functools.partial(relevance_kernel, tile), out_shape=(jax....  3.5 us

profile of v7, /device:TPU:1, one launch (start us, length us, event | category | flops | bytes accessed | tf_op | source)
XLA Modules:
  0.0 36.3 jit_solution(9183753567207405677)
XLA Ops:
  0.6 32.2 %refresh.1 = (bf16[4096,256]{1,0:T(8,128)(2,1)S(1)}, bf16[896,256]{1,0:T(8,128)(2,1)S(1)}, bf16[64,128]{1,0:T(8,128)(2,1)S(1)}) custom-call(s32[64]{0:T(128)} %ws_hbm.1, s32[1,64]{1,0:T(1,128)} %bitcast.11, bf16[7,128,128]{2,1,0:T(8,128)(2,1)} %bitcast.8, bf16[128,128]{1,0:T(8,128)(2,1)} %bitcast.9, bf16[64,128]{1,0:T(8,128)(2,1)} %bitcast.10), custom_call_target="tpu_custom_call" | custom-call | tf_op jit(solution)/shard_map/refresh/pallas_call | solution.py:355
  32.8 3.5 %relevance.1 = (bf16[896,4096]{1,0:T(8,128)(2,1)}, bf16[64,128]{1,0:T(8,128)(2,1)}) custom-call(bf16[896,256]{1,0:T(8,128)(2,1)S(1)} %get-tuple-element.7.lhs, bf16[4096,256]{1,0:T(8,128)(2,1)S(1)} %get-tuple-element.8.rhs, bf16[64,128]{1,0:T(8,128)(2,1)S(1)} %get-tuple-element.9.shard), custom_call_target="tpu_custom_call" | custom-call | tf_op jit(solution)/shard_map/relevance/pallas_call | solution.py:405
